TPU v7x, 32 devices: a 4x4x1 block of a 4x4x8 slice. The times are simulated.
32 devices in a mesh: data: 1 (over z), dap2: 4 (over y), dap: 8 (over x, core).
Axes of the slice: x: 4, y: 4, z: 1, core: 2. Of those that a mesh axis runs over, the one named last changes fastest.
The devices are a block of a 4x4x8 slice.
Arguments:
- pair_act: float32 [384, 384, 128], P(('data', 'dap'), 'dap2')
- pair_mask: int32 [384, 384], P(('data', 'dap'), 'dap2')
- ln_z: bfloat16 [4, 2, 2, 128], replicated
- w_ab: bfloat16 [4, 2, 128, 512], replicated
- w_g: bfloat16 [4, 2, 128, 128], replicated
- ln_x: bfloat16 [4, 2, 2, 128], replicated
- w_o: bfloat16 [4, 2, 128, 128], replicated
Outputs:
- output: float32 [384, 384, 128], P(('data', 'dap'), 'dap2')
All inputs are finite; a program needn't handle non-finite values.
Results may differ from a plain program's by a relative error of at most 0.00360306.
Values are sent between devices in bfloat16 or wider.
A program may use at most 768 MiB of HBM per device.

v0:
```python
import jax
import jax.numpy as jnp
from jax import lax
from jax.sharding import PartitionSpec as P

LN_EPS = 1e-5


def norm_last(values, params):
    mean = jnp.mean(values, axis=-1, keepdims=True)
    centered = values - mean
    variance = jnp.mean(centered * centered, axis=-1, keepdims=True)
    scaled = centered * lax.rsqrt(variance + LN_EPS)
    return (scaled * params[0].astype(jnp.float32) + params[1].astype(jnp.float32)).astype(jnp.bfloat16)


def norm_chan(values, params):
    mean = jnp.mean(values, axis=-3, keepdims=True)
    centered = values - mean
    variance = jnp.mean(centered * centered, axis=-3, keepdims=True)
    scaled = centered * lax.rsqrt(variance + LN_EPS)
    gain = params[0].astype(jnp.float32)[:, None, None]
    bias = params[1].astype(jnp.float32)[:, None, None]
    return (scaled * gain + bias).astype(jnp.bfloat16)


def project_local(z_norm, keep_mask, w_ab):
    hidden = w_ab.shape[1] // 4
    projected = jnp.einsum("ijd,de->eij", z_norm, w_ab, preferred_element_type=jnp.float32)
    a_proj = (keep_mask * jax.nn.sigmoid(projected[hidden:2 * hidden]) * projected[:hidden]).astype(jnp.bfloat16)
    b_proj = (keep_mask * jax.nn.sigmoid(projected[3 * hidden:]) * projected[2 * hidden:3 * hidden]).astype(jnp.bfloat16)
    return a_proj, b_proj


def finish_local(pair_state, z_norm, x_sum, ln_x, w_g, w_o):
    x_norm = norm_chan(x_sum, ln_x)
    update_val = jnp.einsum("cij,cd->ijd", x_norm, w_o, preferred_element_type=jnp.float32)
    gate_val = jax.nn.sigmoid(jnp.einsum("ijd,de->ije", z_norm, w_g, preferred_element_type=jnp.float32))
    return pair_state + gate_val * update_val


def to_transposed(blocks, row_devs, col_devs):
    hidden, n_rows, n_cols = blocks.shape
    n_full = n_rows * row_devs
    fine_rows = n_full // (row_devs * col_devs)
    stage_one = lax.all_to_all(blocks, "dap2", 1, 2, tiled=True)
    stage_one = stage_one.reshape(hidden, fine_rows, row_devs, col_devs * fine_rows)
    stage_two = lax.all_to_all(stage_one, "dap2", 3, 1, tiled=True)
    stage_three = lax.all_to_all(stage_two, "dap", 2, 1, tiled=True)
    stage_three = stage_three.reshape(hidden, n_full, fine_rows)
    return lax.all_to_all(stage_three, "dap2", 1, 2, tiled=True)


def solution(mesh):
    row_devs = mesh.shape["dap"]
    col_devs = mesh.shape["dap2"]
    pair_spec = P(("data", "dap"), "dap2", None)
    mask_spec = P(("data", "dap"), "dap2")

    def tri_update(pair_state, keep_mask, ln_z, w_ab, w_g, ln_x, w_o, outgoing):
        z_norm = norm_last(pair_state, ln_z)
        a_proj, b_proj = project_local(z_norm, keep_mask, w_ab)
        if outgoing:
            a_rows = lax.all_gather(a_proj, "dap2", axis=2, tiled=True)
            b_rows = lax.all_gather(to_transposed(b_proj, row_devs, col_devs), "dap", axis=2, tiled=True)
            x_sum = jnp.einsum("cik,cjk->cij", a_rows, b_rows, preferred_element_type=jnp.float32)
        else:
            a_cols = lax.all_gather(to_transposed(a_proj, row_devs, col_devs), "dap2", axis=1, tiled=True)
            b_cols = lax.all_gather(b_proj, "dap", axis=1, tiled=True)
            x_sum = jnp.einsum("cki,ckj->cij", a_cols, b_cols, preferred_element_type=jnp.float32)
        return finish_local(pair_state, z_norm, x_sum, ln_x, w_g, w_o)

    def local_stack(pair_act, pair_mask, ln_z, w_ab, w_g, ln_x, w_o):
        keep_mask = pair_mask.astype(jnp.float32)
        pair_state = pair_act
        for layer in range(w_o.shape[0]):
            pair_state = tri_update(pair_state, keep_mask, ln_z[layer, 0], w_ab[layer, 0], w_g[layer, 0], ln_x[layer, 0], w_o[layer, 0], True)
            pair_state = tri_update(pair_state, keep_mask, ln_z[layer, 1], w_ab[layer, 1], w_g[layer, 1], ln_x[layer, 1], w_o[layer, 1], False)
        return pair_state

    return jax.shard_map(local_stack, mesh=mesh, in_specs=(pair_spec, mask_spec, P(), P(), P(), P(), P()), out_specs=pair_spec, check_vma=False)
```

profile of v0, /device:TPU:97, one launch (start us, length us, event | category | flops | bytes accessed | tf_op | source)
XLA Modules:
  0.0 1685.9 jit_solution(17779361946497711481)
XLA Ops:
  17.5 27.2 %all_to_all.528 = bf16[128,48,96]{0,2,1:T(8,128)(2,1)S(1)} all-to-all(bf16[128,48,96]{0,2,1:T(8,128)(2,1)S(1)} %get-tuple-element.19), channel_id=1, replica_groups=mesh['data'=1,'dap2'=4,'dap'=8] {'dap2'}, dimensions={1} | all-to-all | bytes 2359296 | tf_op jit(solution)/shard_map/all_to_all | solution.py:46
  45.1 30.5 %all_to_all.529 = bf16[128,12,8,48]{0,2,1,3:T(8,128)(2,1)S(1)} all-to-all(bf16[128,12,8,48]{0,2,1,3:T(8,128)(2,1)S(1)} %copy.189), channel_id=1, replica_groups=mesh['data'=1,'dap2'=4,'dap'=8] {'dap2'}, dimensions={3} | all-to-all | bytes 2359296 | tf_op jit(solution)/shard_map/all_to_all | solution.py:48
  76.3 26.7 %all_to_all.530 = bf16[128,48,8,12]{0,1,3,2:T(8,128)(2,1)S(1)} all-to-all(bf16[128,48,8,12]{0,1,3,2:T(8,128)(2,1)S(1)} %copy.192), channel_id=1, replica_groups=mesh['data'=1,'dap2'=4,'dap'=8] {'dap'}, dimensions={2} | all-to-all | bytes 2359296 | tf_op jit(solution)/shard_map/all_to_all | solution.py:49
  140.5 51.9 %all-gather.19.cloned.1.call-done = bf16[128,96,384]{1,2,0:T(8,128)(2,1)} async-done(((bf16[128,96,48]{1,2,0:T(8,128)(2,1)}), bf16[128,96,384]{1,2,0:T(8,128)(2,1)}) %all-gather.19.cloned.1.call-update) | async-done | bytes 9437200 | tf_op jit(solution)/shard_map/all_gather | solution.py:65
  302.4 44.0 %all-gather.21.cloned.1.call-done = bf16[128,384,48]{0,2,1:T(8,128)(2,1)} async-done(((bf16[128,96,48]{0,2,1:T(8,128)(2,1)}), bf16[128,384,48]{0,2,1:T(8,128)(2,1)}) %all-gather.21.cloned.1.call-update) | async-done | bytes 4718608 | tf_op jit(solution)/shard_map/all_gather | solution.py:68
  354.1 46.2 %all-gather.23.cloned.1.call-done = bf16[128,384,96]{0,2,1:T(8,128)(2,1)} async-done(((bf16[128,48,96]{0,2,1:T(8,128)(2,1)}), bf16[128,384,96]{0,2,1:T(8,128)(2,1)}) %all-gather.23.cloned.1.call-update) | async-done | bytes 9437200 | tf_op jit(solution)/shard_map/all_gather | solution.py:69
  435.5 27.3 %all_to_all.536 = bf16[128,48,96]{0,2,1:T(8,128)(2,1)S(1)} all-to-all(bf16[128,48,96]{0,2,1:T(8,128)(2,1)S(1)} %get-tuple-element.15), channel_id=1, replica_groups=mesh['data'=1,'dap2'=4,'dap'=8] {'dap2'}, dimensions={1} | all-to-all | bytes 2359296 | tf_op jit(solution)/shard_map/all_to_all | solution.py:46
  463.3 30.6 %all_to_all.537 = bf16[128,12,8,48]{0,2,1,3:T(8,128)(2,1)S(1)} all-to-all(bf16[128,12,8,48]{0,2,1,3:T(8,128)(2,1)S(1)} %copy.214), channel_id=1, replica_groups=mesh['data'=1,'dap2'=4,'dap'=8] {'dap2'}, dimensions={3} | all-to-all | bytes 2359296 | tf_op jit(solution)/shard_map/all_to_all | solution.py:48
  494.5 23.9 %all_to_all.538 = bf16[128,48,8,12]{0,1,3,2:T(8,128)(2,1)S(1)} all-to-all(bf16[128,48,8,12]{0,1,3,2:T(8,128)(2,1)S(1)} %copy.217), channel_id=1, replica_groups=mesh['data'=1,'dap2'=4,'dap'=8] {'dap'}, dimensions={2} | all-to-all | bytes 2359296 | tf_op jit(solution)/shard_map/all_to_all | solution.py:49
  555.5 52.5 %all-gather.27.cloned.1.call-done = bf16[128,96,384]{1,2,0:T(8,128)(2,1)} async-done(((bf16[128,96,48]{1,2,0:T(8,128)(2,1)}), bf16[128,96,384]{1,2,0:T(8,128)(2,1)}) %all-gather.27.cloned.1.call-update) | async-done | bytes 9437200 | tf_op jit(solution)/shard_map/all_gather | solution.py:65
  718.7 43.8 %all-gather.29.cloned.1.call-done = bf16[128,384,48]{0,2,1:T(8,128)(2,1)} async-done(((bf16[128,96,48]{0,2,1:T(8,128)(2,1)}), bf16[128,384,48]{0,2,1:T(8,128)(2,1)}) %all-gather.29.cloned.1.call-update) | async-done | bytes 4718608 | tf_op jit(solution)/shard_map/all_gather | solution.py:68
  770.2 46.4 %all-gather.31.cloned.1.call-done = bf16[128,384,96]{0,2,1:T(8,128)(2,1)} async-done(((bf16[128,48,96]{0,2,1:T(8,128)(2,1)}), bf16[128,384,96]{0,2,1:T(8,128)(2,1)}) %all-gather.31.cloned.1.call-update) | async-done | bytes 9437200 | tf_op jit(solution)/shard_map/all_gather | solution.py:69
  851.9 28.1 %all_to_all.544 = bf16[128,48,96]{0,2,1:T(8,128)(2,1)S(1)} all-to-all(bf16[128,48,96]{0,2,1:T(8,128)(2,1)S(1)} %get-tuple-element.11), channel_id=1, replica_groups=mesh['data'=1,'dap2'=4,'dap'=8] {'dap2'}, dimensions={1} | all-to-all | bytes 2359296 | tf_op jit(solution)/shard_map/all_to_all | solution.py:46
  880.5 30.6 %all_to_all.545 = bf16[128,12,8,48]{0,2,1,3:T(8,128)(2,1)S(1)} all-to-all(bf16[128,12,8,48]{0,2,1,3:T(8,128)(2,1)S(1)} %copy.239), channel_id=1, replica_groups=mesh['data'=1,'dap2'=4,'dap'=8] {'dap2'}, dimensions={3} | all-to-all | bytes 2359296 | tf_op jit(solution)/shard_map/all_to_all | solution.py:48
  911.7 23.5 %all_to_all.546 = bf16[128,48,8,12]{0,1,3,2:T(8,128)(2,1)S(1)} all-to-all(bf16[128,48,8,12]{0,1,3,2:T(8,128)(2,1)S(1)} %copy.242), channel_id=1, replica_groups=mesh['data'=1,'dap2'=4,'dap'=8] {'dap'}, dimensions={2} | all-to-all | bytes 2359296 | tf_op jit(solution)/shard_map/all_to_all | solution.py:49
  972.2 52.5 %all-gather.35.cloned.1.call-done = bf16[128,96,384]{1,2,0:T(8,128)(2,1)} async-done(((bf16[128,96,48]{1,2,0:T(8,128)(2,1)}), bf16[128,96,384]{1,2,0:T(8,128)(2,1)}) %all-gather.35.cloned.1.call-update) | async-done | bytes 9437200 | tf_op jit(solution)/shard_map/all_gather | solution.py:65
  1135.5 44.0 %all-gather.37.cloned.1.call-done = bf16[128,384,48]{0,2,1:T(8,128)(2,1)} async-done(((bf16[128,96,48]{0,2,1:T(8,128)(2,1)}), bf16[128,384,48]{0,2,1:T(8,128)(2,1)}) %all-gather.37.cloned.1.call-update) | async-done | bytes 4718608 | tf_op jit(solution)/shard_map/all_gather | solution.py:68
  1187.2 46.2 %all-gather.39.cloned.1.call-done = bf16[128,384,96]{0,2,1:T(8,128)(2,1)} async-done(((bf16[128,48,96]{0,2,1:T(8,128)(2,1)}), bf16[128,384,96]{0,2,1:T(8,128)(2,1)}) %all-gather.39.cloned.1.call-update) | async-done | bytes 9437200 | tf_op jit(solution)/shard_map/all_gather | solution.py:69
  1268.8 27.3 %all_to_all.552 = bf16[128,48,96]{0,2,1:T(8,128)(2,1)S(1)} all-to-all(bf16[128,48,96]{0,2,1:T(8,128)(2,1)S(1)} %get-tuple-element.7), channel_id=1, replica_groups=mesh['data'=1,'dap2'=4,'dap'=8] {'dap2'}, dimensions={1} | all-to-all | bytes 2359296 | tf_op jit(solution)/shard_map/all_to_all | solution.py:46
  1296.6 30.6 %all_to_all.553 = bf16[128,12,8,48]{0,2,1,3:T(8,128)(2,1)S(1)} all-to-all(bf16[128,12,8,48]{0,2,1,3:T(8,128)(2,1)S(1)} %copy.264), channel_id=1, replica_groups=mesh['data'=1,'dap2'=4,'dap'=8] {'dap2'}, dimensions={3} | all-to-all | bytes 2359296 | tf_op jit(solution)/shard_map/all_to_all | solution.py:48
  1327.8 23.7 %all_to_all.554 = bf16[128,48,8,12]{0,1,3,2:T(8,128)(2,1)S(1)} all-to-all(bf16[128,48,8,12]{0,1,3,2:T(8,128)(2,1)S(1)} %copy.267), channel_id=1, replica_groups=mesh['data'=1,'dap2'=4,'dap'=8] {'dap'}, dimensions={2} | all-to-all | bytes 2359296 | tf_op jit(solution)/shard_map/all_to_all | solution.py:49
  1388.6 52.5 %all-gather.43.cloned.1.call-done = bf16[128,96,384]{1,2,0:T(8,128)(2,1)} async-done(((bf16[128,96,48]{1,2,0:T(8,128)(2,1)}), bf16[128,96,384]{1,2,0:T(8,128)(2,1)}) %all-gather.43.cloned.1.call-update) | async-done | bytes 9437200 | tf_op jit(solution)/shard_map/all_gather | solution.py:65
  1551.5 44.0 %all-gather.45.cloned.1.call-done = bf16[128,384,48]{0,2,1:T(8,128)(2,1)} async-done(((bf16[128,96,48]{0,2,1:T(8,128)(2,1)}), bf16[128,384,48]{0,2,1:T(8,128)(2,1)}) %all-gather.45.cloned.1.call-update) | async-done | bytes 4718608 | tf_op jit(solution)/shard_map/all_gather | solution.py:68
  1603.3 46.2 %all-gather.47.cloned.1.call-done = bf16[128,384,96]{0,2,1:T(8,128)(2,1)} async-done(((bf16[128,48,96]{0,2,1:T(8,128)(2,1)}), bf16[128,384,96]{0,2,1:T(8,128)(2,1)}) %all-gather.47.cloned.1.call-update) | async-done | bytes 9437200 | tf_op jit(solution)/shard_map/all_gather | solution.py:69
  (352 shorter events, 770.1 us)
Async XLA Ops:
  6.5 4.2 copy-start
  6.5 126.8 %all-gather.17.cloned.1.call-start = ((), (), s32[]{:S(2)}) async-start(), calls=%async_computation.32 | async-start | bytes 5898240 | tf_op jit(solution)/shard_map/all_gather | solution.py:64
  8.1 4.3 copy-start.46
  8.2 4.3 copy-start.47
  8.2 4.3 copy-start.33
  10.8 4.1 copy-start.25
  17.4 175.0 %all-gather.19.cloned.1.call-start = ((), (), s32[]{:S(2)}) async-start(), calls=%async_computation.33 | async-start | bytes 14155776 | tf_op jit(solution)/shard_map/all_gather | solution.py:65
  128.3 218.1 %all-gather.21.cloned.1.call-start = ((), (), s32[]{:S(2)}) async-start(), calls=%async_computation.34 | async-start | bytes 5898240 | tf_op jit(solution)/shard_map/all_gather | solution.py:68
  205.3 4.1 copy-start.1
  297.8 102.6 %all-gather.23.cloned.1.call-start = ((), (), s32[]{:S(2)}) async-start(), calls=%async_computation.35 | async-start | bytes 10616832 | tf_op jit(solution)/shard_map/all_gather | solution.py:69
  298.4 250.0 %all-gather.25.cloned.1.call-start = ((), (), s32[]{:S(2)}) async-start(), calls=%async_computation.36 | async-start | bytes 5898240 | tf_op jit(solution)/shard_map/all_gather | solution.py:64
  435.4 172.5 %all-gather.27.cloned.1.call-start = ((), (), s32[]{:S(2)}) async-start(), calls=%async_computation.37 | async-start | bytes 14155776 | tf_op jit(solution)/shard_map/all_gather | solution.py:65
  543.9 218.6 %all-gather.29.cloned.1.call-start = ((), (), s32[]{:S(2)}) async-start(), calls=%async_computation.38 | async-start | bytes 5898240 | tf_op jit(solution)/shard_map/all_gather | solution.py:68
  713.9 102.7 %all-gather.31.cloned.1.call-start = ((), (), s32[]{:S(2)}) async-start(), calls=%async_computation.39 | async-start | bytes 10616832 | tf_op jit(solution)/shard_map/all_gather | solution.py:69
  714.7 250.4 %all-gather.33.cloned.1.call-start = ((), (), s32[]{:S(2)}) async-start(), calls=%async_computation.40 | async-start | bytes 5898240 | tf_op jit(solution)/shard_map/all_gather | solution.py:64
  845.2 4.1 copy-start.6
  851.8 172.9 %all-gather.35.cloned.1.call-start = ((), (), s32[]{:S(2)}) async-start(), calls=%async_computation.41 | async-start | bytes 14155776 | tf_op jit(solution)/shard_map/all_gather | solution.py:65
  960.7 218.9 %all-gather.37.cloned.1.call-start = ((), (), s32[]{:S(2)}) async-start(), calls=%async_computation.42 | async-start | bytes 5898240 | tf_op jit(solution)/shard_map/all_gather | solution.py:68
  1130.9 102.6 %all-gather.39.cloned.1.call-start = ((), (), s32[]{:S(2)}) async-start(), calls=%async_computation.43 | async-start | bytes 10616832 | tf_op jit(solution)/shard_map/all_gather | solution.py:69
  1131.5 250.0 %all-gather.41.cloned.1.call-start = ((), (), s32[]{:S(2)}) async-start(), calls=%async_computation.44 | async-start | bytes 5898240 | tf_op jit(solution)/shard_map/all_gather | solution.py:64
  1262.1 4.1 copy-start.9
  1268.7 172.3 %all-gather.43.cloned.1.call-start = ((), (), s32[]{:S(2)}) async-start(), calls=%async_computation.45 | async-start | bytes 14155776 | tf_op jit(solution)/shard_map/all_gather | solution.py:65
  1377.0 218.6 %all-gather.45.cloned.1.call-start = ((), (), s32[]{:S(2)}) async-start(), calls=%async_computation.46 | async-start | bytes 5898240 | tf_op jit(solution)/shard_map/all_gather | solution.py:68
  1546.9 102.6 %all-gather.47.cloned.1.call-start = ((), (), s32[]{:S(2)}) async-start(), calls=%async_computation.47 | async-start | bytes 10616832 | tf_op jit(solution)/shard_map/all_gather | solution.py:69
  (52 other events, 96.0 us)
Sparse Core Ops, SparseCore 0:
  17.5 73.6 all-gather.16
  128.5 63.9 all-gather.18
  297.9 48.4 all-gather.20
  347.9 52.4 all-gather.22
  435.6 71.1 all-gather.24
  544.0 63.8 all-gather.26
  714.0 48.4 all-gather.28
  764.1 52.4 all-gather.30
  852.0 71.5 all-gather.32
  960.8 63.8 all-gather.34
  1131.0 48.4 all-gather.36
  1181.0 52.4 all-gather.38
  1268.9 71.1 all-gather.40
  1377.1 63.8 all-gather.42
  1547.1 48.4 all-gather.44
  1597.0 52.4 all-gather.46
where the time goes:
time: 1700 us; the launch traced here: 1690 us
  blocking collectives  747 us (44%)
  waiting for transfers between devices  573 us (34%)
  local copies, waits for them, and re-layouts  166 us (10%)
  matrix products  138 us (8%)
  other arithmetic  46.3 us (3%)
    all_gather x4, waiting for transfers between devices, tri_update(): lax.all_gather(to_transposed(b_proj, row_devs, col_devs), 'dap', axis=2,...  209 us
    all_to_all x8, blocking collectives, to_transposed(): stage_two = lax.all_to_all(stage_one, 'dap2', 3, 1, tiled=True)  192 us
    all_to_all x8, blocking collectives, to_transposed(): stage_one = lax.all_to_all(blocks, 'dap2', 1, 2, tiled=True)  190 us
    all_to_all x8, blocking collectives, to_transposed(): stage_three = lax.all_to_all(stage_two, 'dap', 2, 1, tiled=True)  187 us
    all_gather x4, waiting for transfers between devices, tri_update(): b_cols = lax.all_gather(b_proj, 'dap', axis=1, tiled=True)  185 us
    all_to_all x8, blocking collectives, to_transposed(): return lax.all_to_all(stage_three, 'dap2', 1, 2, tiled=True)  178 us
    all_gather x4, waiting for transfers between devices, tri_update(): lax.all_gather(to_transposed(a_proj, row_devs, col_devs), 'dap2', axis=1,...  176 us
    all_gather x4, local copies, waits for them, and re-layouts, tri_update(): b_cols = lax.all_gather(b_proj, 'dap', axis=1, tiled=True)  62.2 us
  transfers between devices with their start and end apart: 16, of which 12 were waited for; matrix products, arithmetic and copies ran while one was open for 6% of the time, Pallas kernels for 0%

commit v1 on v0

v1 whole, which is shorter than its diff:
```python
import functools

import jax
import jax.numpy as jnp
from jax import lax
from jax.experimental import pallas as pl
from jax.experimental.pallas import tpu as pltpu
from jax.sharding import PartitionSpec as P

LN_EPS = 1e-5
LANES = 128
GROUPS = 4
TILES = 3
MESH = pl.DeviceIdType.MESH


def lane_iota(shape):
    return lax.broadcasted_iota(jnp.int32, shape, len(shape) - 1)


def pack_tiles(blocks, cols):
    part = LANES - cols
    lane = lane_iota(blocks[0].shape)
    return [jnp.where(lane < cols, blocks[t], pltpu.roll(blocks[3], cols - part * t, 1)) for t in range(TILES)]


def last_group(tiles, cols):
    part = LANES - cols
    lane = lane_iota(tiles[0].shape)
    moved = [pltpu.roll(tiles[t], part * (t + 1), 1) for t in range(TILES)]
    return jnp.where(lane < part, moved[0], jnp.where(lane < 2 * part, moved[1], moved[2]))


def norm_sublanes(values, gain, bias):
    mean = jnp.mean(values, axis=0, keepdims=True)
    centered = values - mean
    variance = jnp.mean(centered * centered, axis=0, keepdims=True)
    return (centered * lax.rsqrt(variance + LN_EPS) * gain + bias).astype(jnp.bfloat16)


def kernel(n_dap, n_dap2, n_updates, z_ref, m_ref, w_ref, ln_ref, out_ref, zt, zn, stage, send, recv, xs, xr, lnb,
           send_sem, recv_sem, xsend_sem, xrecv_sem):
    rows, cols, width = z_ref.shape
    n_all = n_dap * n_dap2
    pitch = stage.shape[2] // n_all
    per = width // GROUPS
    full = rows * n_dap
    my_p, my_q = lax.axis_index("dap"), lax.axis_index("dap2")
    me = my_p * n_dap2 + my_q

    barrier = pltpu.get_barrier_semaphore()

    @pl.loop(1, n_all)
    def _(off):
        peer = lax.rem(me + off, n_all)
        pl.semaphore_signal(barrier, inc=1, device_id={"dap": peer // n_dap2, "dap2": lax.rem(peer, n_dap2)}, device_id_type=MESH)

    pl.semaphore_wait(barrier, n_all - 1)

    def load_params(update):
        for k in range(4):
            lnb[k] = jnp.broadcast_to(ln_ref[update, :, k:k + 1], (width, LANES))

    def project_row(i, update):
        n_row = norm_sublanes(zt[i], lnb[0], lnb[1])
        zn[i] = n_row
        keep = m_ref[pl.ds(i, 1), :]
        a_blocks, b_blocks = [], []
        for g in range(GROUPS):
            q = jnp.dot(w_ref[update, g * 4 * per:(g + 1) * 4 * per, :], n_row, preferred_element_type=jnp.float32)
            a_blocks.append(jax.nn.sigmoid(q[per:2 * per]) * q[:per] * keep)
            b_blocks.append(jax.nn.sigmoid(q[3 * per:]) * q[2 * per:3 * per] * keep)
        for side, blocks in enumerate((a_blocks, b_blocks)):
            for t, tile in enumerate(pack_tiles(blocks, cols)):
                stage[side, t, pl.ds(i, n_all, stride=pitch), :] = tile

    def finish_row(i, update):
        tiles = [xr[t, pl.ds(i, n_all, stride=pitch), :] for t in range(TILES)]
        x_row = jnp.concatenate([*tiles, last_group(tiles, cols)], axis=0)
        x_norm = norm_sublanes(x_row, lnb[2], lnb[3])
        gate = jnp.dot(w_ref[update, 4 * width:5 * width, :], zn[i], preferred_element_type=jnp.float32)
        value = jnp.dot(w_ref[update, 5 * width:6 * width, :], x_norm, preferred_element_type=jnp.float32)
        zt[i] = zt[i] + jax.nn.sigmoid(gate) * value

    def pack_sends():
        @pl.loop(0, n_all)
        def _(g):
            for side in range(2):
                for t in range(TILES):
                    send[g, side, t] = stage[side, t, pl.ds(pl.multiple_of(g * pitch, 8), rows), :].astype(jnp.bfloat16)

    def ab_slot(parity):
        return recv.at[parity, :, :, pl.ds(pl.multiple_of(my_p * rows, 16), rows), pl.ds(pl.multiple_of(my_q * LANES, LANES), LANES)]

    def x_slots(p, q):
        return xs.at[q, :, pl.ds(pl.multiple_of(p * rows, 8), rows), :], xr.at[:, pl.ds(pl.multiple_of(me * pitch, 8), rows), :]

    def ab_copy(peer, parity):
        return pltpu.make_async_remote_copy(
            src_ref=send.at[peer],
            dst_ref=ab_slot(parity),
            send_sem=send_sem, recv_sem=recv_sem.at[parity],
            device_id={"dap": peer // n_dap2, "dap2": lax.rem(peer, n_dap2)}, device_id_type=MESH)

    def x_copy(peer):
        p, q = peer // n_dap2, lax.rem(peer, n_dap2)
        src, dst = x_slots(p, q)
        return pltpu.make_async_remote_copy(
            src_ref=src,
            dst_ref=dst,
            send_sem=xsend_sem, recv_sem=xrecv_sem,
            device_id={"dap": p, "dap2": q}, device_id_type=MESH)

    def wait_bytes(ref, sem):
        pltpu.make_async_copy(ref, ref, sem).wait()

    def exchange(parity):
        kept = pltpu.make_async_copy(send.at[me], ab_slot(parity), recv_sem.at[parity])
        kept.start()

        @pl.loop(1, n_all)
        def _(off):
            ab_copy(lax.rem(me + off, n_all), parity).start()

        wait_bytes(recv.at[parity], recv_sem.at[parity])

    def store_x(q, row, blocks):
        for t, tile in enumerate(pack_tiles(blocks, cols)):
            xs[q, t, pl.ds(row, cols), :] = tile

    def contract_outgoing(parity):
        @pl.loop(0, full // cols)
        def _(chunk):
            row = pl.multiple_of(chunk * cols, 16)
            lane = lax.rem(lane_iota((cols, n_dap2 * LANES)), LANES)
            a_tiles = [recv[parity, 0, t, pl.ds(row, cols), :] for t in range(TILES)]
            zero = jnp.zeros_like(a_tiles[0])
            low = [jnp.where(lane < cols, a, zero) for a in a_tiles]
            high = [jnp.where(lane < cols, zero, a) for a in a_tiles]

            @pl.loop(0, n_dap2)
            def _(q):
                b_tiles = [recv[parity, 1, t, pl.ds(pl.multiple_of(q * cols, 16), cols), :] for t in range(TILES)]

                def dot(a, b):
                    x = lax.dot_general(a, b, (((1,), (1,)), ((), ())), preferred_element_type=jnp.float32)
                    return jnp.concatenate([x, jnp.zeros((cols, LANES - cols), jnp.float32)], axis=1)

                blocks = [dot(low[t], b_tiles[t]) for t in range(TILES)]
                blocks.append(dot(high[0], b_tiles[0]) + dot(high[1], b_tiles[1]) + dot(high[2], b_tiles[2]))
                store_x(q, row, blocks)

    def contract_incoming(parity):
        def tiles_of(side, q):
            lanes = pl.ds(pl.multiple_of(q * LANES, LANES), LANES)
            tiles = [recv[parity, side, t, :, lanes] for t in range(TILES)]
            fourth = last_group([tile.astype(jnp.float32) for tile in tiles], cols).astype(jnp.bfloat16)
            return [*tiles, fourth]

        @pl.loop(0, n_dap2)
        def _(qi):
            a_all = [a.T[:cols] for a in tiles_of(0, qi)]

            @pl.loop(0, n_dap2)
            def _(qj):
                blocks = [jnp.dot(a, b, preferred_element_type=jnp.float32) for a, b in zip(a_all, tiles_of(1, qj))]
                store_x(qj, pl.multiple_of(qi * cols, 8), blocks)

    def send_x():
        kept = pltpu.make_async_copy(*x_slots(my_p, my_q), xrecv_sem)
        kept.start()

        @pl.loop(1, n_all)
        def _(off):
            x_copy(lax.rem(me + off, n_all)).start()

    def one_update(update, parity, contract, last):
        pack_sends()
        exchange(parity)
        contract(parity)
        wait_bytes(send.at[pl.ds(0, n_all - 1)], send_sem)
        send_x()
        wait_bytes(xs, xrecv_sem)
        wait_bytes(xr.at[:, pl.ds(0, (n_all - 1) * rows), :], xsend_sem)

        @pl.loop(0, rows)
        def _(i):
            finish_row(i, update)

        load_params(jnp.minimum(update + 1, n_updates - 1))

        @pl.loop(0, rows)
        def _(i):
            project_row(i, jnp.minimum(update + 1, n_updates - 1))

    @pl.loop(0, rows)
    def _(i):
        zt[i] = jnp.zeros((width, LANES), jnp.float32)
        zt[i, :, :cols] = z_ref[i].T

    load_params(0)

    @pl.loop(0, rows)
    def _(i):
        project_row(i, 0)

    @pl.loop(0, n_updates // 2)
    def _(layer):
        one_update(2 * layer, 0, contract_outgoing, False)
        one_update(2 * layer + 1, 1, contract_incoming, False)

    @pl.loop(0, rows)
    def _(i):
        out_ref[i] = zt[i].T[:cols]


def solution(mesh):
    n_dap, n_dap2 = mesh.shape["dap"], mesh.shape["dap2"]
    n_all = n_dap * n_dap2
    pair_spec = P(("data", "dap"), "dap2", None)
    mask_spec = P(("data", "dap"), "dap2")

    def local_stack(pair_act, pair_mask, ln_z, w_ab, w_g, ln_x, w_o):
        rows, cols, width = pair_act.shape
        n_updates = w_o.shape[0] * w_o.shape[1]
        per = width // GROUPS
        full = rows * n_dap
        pitch = rows + 8
        mask = jnp.pad(pair_mask.astype(jnp.float32), ((0, 0), (0, LANES - cols)))
        w_ab = w_ab.reshape(n_updates, width, 4, GROUPS, per).transpose(0, 3, 2, 4, 1).reshape(n_updates, 4 * width, width)
        w_g = w_g.reshape(n_updates, width, width).transpose(0, 2, 1)
        w_o = w_o.reshape(n_updates, width, width).transpose(0, 2, 1)
        weights = jnp.concatenate([w_ab, w_g, w_o], axis=1)
        norms = jnp.concatenate([ln_z, ln_x], axis=2).reshape(n_updates, 4, width).transpose(0, 2, 1).astype(jnp.float32)
        vmem = pl.BlockSpec(memory_space=pltpu.VMEM)
        return pl.pallas_call(
            functools.partial(kernel, n_dap, n_dap2, n_updates),
            out_shape=jax.ShapeDtypeStruct((rows, cols, width), jnp.float32),
            in_specs=[vmem] * 4,
            out_specs=vmem,
            scratch_shapes=[
                pltpu.VMEM((rows, width, LANES), jnp.float32),
                pltpu.VMEM((rows, width, LANES), jnp.bfloat16),
                pltpu.VMEM((2, TILES, n_all * pitch, LANES), jnp.float32),
                pltpu.VMEM((n_all, 2, TILES, rows, LANES), jnp.bfloat16),
                pltpu.VMEM((2, 2, TILES, full, n_dap2 * LANES), jnp.bfloat16),
                pltpu.VMEM((n_dap2, TILES, full, LANES), jnp.float32),
                pltpu.VMEM((TILES, n_all * pitch, LANES), jnp.float32),
                pltpu.VMEM((4, width, LANES), jnp.float32),
                pltpu.SemaphoreType.DMA,
                pltpu.SemaphoreType.DMA((2,)),
                pltpu.SemaphoreType.DMA,
                pltpu.SemaphoreType.DMA,
            ],
            compiler_params=pltpu.CompilerParams(collective_id=0, has_side_effects=True, vmem_limit_bytes=60 * 1024 * 1024),
            name="triangle_stack",
        )(pair_act, mask, weights, norms)

    return jax.shard_map(local_stack, mesh=mesh, in_specs=(pair_spec, mask_spec, P(), P(), P(), P(), P()), out_specs=pair_spec, check_vma=False)
```

time: 1700 us -> 802 us (0.47)
  Pallas kernels: 0 us -> 791 us
  blocking collectives: 747 us -> 0 us
  waiting for transfers between devices: 573 us -> 0 us
  local copies, waits for them, and re-layouts: 166 us -> 7.9 us
  matrix products: 138 us -> 0 us
  other arithmetic: 46.3 us -> 2.8 us
    pallas_call x0 -> x1, Pallas kernels: none -> 791 us  [local_stack(): pl.pallas_call(functools.partial(kernel, n_dap, n_dap2, n_updates), out_s...]
    all_to_all x32 -> x0, blocking collectives: 747 us -> none  [the longest x8 192 us: to_transposed(): stage_two = lax.all_to_all(stage_one, 'dap2', 3, 1, tiled=True)]
    all_gather x16 -> x0, waiting for transfers between devices: 570 us -> none  [the longest x4 209 us: tri_update(): lax.all_gather(to_transposed(b_proj, row_devs, col_devs), 'dap', axis=2,...]
    dot_general x32 -> x0, matrix products: 138 us -> none  [the longest x4 33.5 us: tri_update(): jnp.einsum('cik,cjk->cij', a_rows, b_rows, preferred_element_type=jnp.flo...]
    all_gather x12 -> x0, local copies, waits for them, and re-layouts: 122 us -> none  [the longest x4 62.2 us: tri_update(): b_cols = lax.all_gather(b_proj, 'dap', axis=1, tiled=True)]
    convert_element_type x19 -> x2, other arithmetic: 26.5 us -> 1.55 us  [the longest x1 0.8 us: local_stack(): jnp.concatenate([ln_z, ln_x], axis=2).reshape(n_updates, 4, width)]
    all_to_all x48 -> x0, local copies, waits for them, and re-layouts: 22.7 us -> none  [the longest x16 15.7 us: to_transposed(): return lax.all_to_all(stage_three, 'dap2', 1, 2, tiled=True)]
    reduce_sum x17 -> x0, other arithmetic: 19.5 us -> none  [the longest x8 13.2 us: norm_last(): variance = jnp.mean(centered * centered, axis=-1, keepdims=True)]
  transfers between devices with their start and end apart: 16 -> 0, of which waited for: 12 -> 0; matrix products, arithmetic and copies ran while one was open for 6% -> 0% of each run, Pallas kernels for 0% -> 0%
where the time goes in v1:
time: 802 us
  Pallas kernels  791 us (99%)
    pallas_call x1, Pallas kernels, local_stack(): pl.pallas_call(functools.partial(kernel, n_dap, n_dap2, n_updates), out_s...  791 us

profile of v1, /device:TPU:97, one launch (start us, length us, event | category | flops | bytes accessed | tf_op | source)
XLA Modules:
  0.0 802.0 jit_solution(607230352872175451)
XLA Ops:
  0.0 0.0 copy-start
  0.0 0.8 maximum_convert_fusion
  0.8 0.7 convert_element_type.12
  1.6 0.6 pad.4.m_ref
  2.2 1.1 copy.14
  3.3 1.1 copy.15
  4.4 1.1 copy.16
  5.5 0.0 copy-done
  5.5 0.7 copy.12
  6.1 0.1 copy.13
  6.3 1.3 pad_maximum_fusion.w_ref
  7.5 791.3 %triangle_stack.1 = f32[48,96,128]{2,1,0:T(8,128)} custom-call(f32[48,96,128]{2,1,0:T(8,128)} %z_ref.1, f32[48,128]{1,0:T(8,128)} %pad.4.m_ref, bf16[8,768,128]{2,1,0:T(8,128)(2,1)} %pad_maximum_fusion.w_ref, f32[8,128,4]{2,1,0:T(8,128)} %bitcast.15), custom_call_target="tpu_custom_call" | custom-call | tf_op jit(solution)/shard_map/triangle_stack/pallas_call | solution.py:236
  798.8 3.2 copy.18
Async XLA Ops:
  0.0 5.5 copy-start

commit v2 on v1

v2 whole, which is shorter than its diff:
```python
import functools

import jax
import jax.numpy as jnp
from jax import lax
from jax.experimental import pallas as pl
from jax.experimental.pallas import tpu as pltpu
from jax.sharding import PartitionSpec as P

LN_EPS = 1e-5
LANES = 128
GROUPS = 4
TILES = 3
CHUNK = 16
UNROLL = 2
MESH = pl.DeviceIdType.MESH


def lane_iota(shape):
    return lax.broadcasted_iota(jnp.int32, shape, len(shape) - 1)


def pack_tiles(blocks, cols):
    part = LANES - cols
    lane = lane_iota(blocks[0].shape)
    return [jnp.where(lane < cols, blocks[t], pltpu.roll(blocks[3], cols - part * t, 1)) for t in range(TILES)]


def last_group(tiles, cols):
    part = LANES - cols
    lane = lane_iota(tiles[0].shape)
    moved = [pltpu.roll(tiles[t], part * (t + 1), 1) for t in range(TILES)]
    return jnp.where(lane < part, moved[0], jnp.where(lane < 2 * part, moved[1], moved[2]))


def norm_sublanes(values, gain, bias):
    mean = jnp.mean(values, axis=0, keepdims=True)
    centered = values - mean
    variance = jnp.mean(centered * centered, axis=0, keepdims=True)
    return (centered * lax.rsqrt(variance + LN_EPS) * gain + bias).astype(jnp.bfloat16)


def kernel(n_dap, n_dap2, n_updates, z_ref, m_ref, w_ref, ln_ref, out_ref, zt, zn, stage, send, recv, at, bl, xs, xr, lnb,
           send_sem, recv_sem, xsend_sem, xrecv_sem):
    rows, cols, width = z_ref.shape
    n_all = n_dap * n_dap2
    pitch, stage_pitch = xr.shape[1] // n_all, stage.shape[2] // n_all
    per = width // GROUPS
    full = rows * n_dap
    n_chunks = rows // CHUNK
    my_p, my_q = lax.axis_index("dap"), lax.axis_index("dap2")
    me = my_p * n_dap2 + my_q

    barrier = pltpu.get_barrier_semaphore()

    @pl.loop(1, n_all)
    def _(off):
        peer = lax.rem(me + off, n_all)
        pl.semaphore_signal(barrier, inc=1, device_id={"dap": peer // n_dap2, "dap2": lax.rem(peer, n_dap2)}, device_id_type=MESH)

    def load_params(first, update):
        for k in (first, first + 1):
            lnb[k] = jnp.broadcast_to(ln_ref[update, :, k:k + 1], (width, LANES))

    def project_rows(indices, local, states, update):
        normed = [norm_sublanes(state, lnb[0], lnb[1]) for state in states]
        for i, n_row in zip(indices, normed):
            zn[i] = n_row
        keeps = [m_ref[pl.ds(i, 1), :] for i in indices]
        blocks = [([], []) for _ in indices]
        for g in range(GROUPS):
            weight = w_ref[update, g * 4 * per:(g + 1) * 4 * per, :]
            for keep, n_row, (a_blocks, b_blocks) in zip(keeps, normed, blocks):
                q = jnp.dot(weight, n_row, preferred_element_type=jnp.float32)
                a_blocks.append(jax.nn.sigmoid(q[per:2 * per]) * q[:per] * keep)
                b_blocks.append(jax.nn.sigmoid(q[3 * per:]) * q[2 * per:3 * per] * keep)
        for k, sides in zip(local, blocks):
            for side in range(2):
                for t, tile in enumerate(pack_tiles(sides[side], cols)):
                    stage[side, t, pl.ds(k, n_all, stride=stage_pitch), :] = tile

    def finish_rows(indices, update):
        tiles = [[xr[t, pl.ds(i, n_all, stride=pitch), :] for t in range(TILES)] for i in indices]
        x_rows = [jnp.concatenate([*tile, last_group(tile, cols)], axis=0) for tile in tiles]
        gates = [jnp.dot(w_ref[update, 4 * width:5 * width, :], zn[i], preferred_element_type=jnp.float32) for i in indices]
        normed = [norm_sublanes(x_row, lnb[2], lnb[3]) for x_row in x_rows]
        values = [jnp.dot(w_ref[update, 5 * width:6 * width, :], x_norm, preferred_element_type=jnp.float32) for x_norm in normed]
        return [zt[i] + jax.nn.sigmoid(gate) * value for i, gate, value in zip(indices, gates, values)]

    def for_rows(r, body):
        @pl.loop(0, CHUNK // UNROLL)
        def _(k):
            local = [k * UNROLL + s for s in range(UNROLL)]
            body([r * CHUNK + i for i in local], local)

    def coords(peer):
        return {"dap": peer // n_dap2, "dap2": lax.rem(peer, n_dap2)}

    def chunk_rows(p, r):
        return pl.ds(pl.multiple_of(p * rows + r * CHUNK, CHUNK), CHUNK)

    def wait_bytes(ref, sem):
        pltpu.make_async_copy(ref, ref, sem).wait()

    def send_chunk(r, parity):
        @pl.loop(0, n_all)
        def _(g):
            for side in range(2):
                for t in range(TILES):
                    send[r, g, side, t] = stage[side, t, pl.ds(pl.multiple_of(g * stage_pitch, 8), CHUNK), :].astype(jnp.bfloat16)

        slot = recv.at[parity, :, :, chunk_rows(my_p, r), pl.ds(pl.multiple_of(my_q * LANES, LANES), LANES)]
        pltpu.make_async_copy(send.at[r, me], slot, recv_sem.at[parity, r]).start()

        @pl.loop(1, n_all)
        def _(off):
            peer = lax.rem(me + off, n_all)
            pltpu.make_async_remote_copy(src_ref=send.at[r, peer], dst_ref=slot, send_sem=send_sem.at[r], recv_sem=recv_sem.at[parity, r],
                                         device_id=coords(peer), device_id_type=MESH).start()

    def send_x(r):
        def slots(p, q):
            return (xs.at[q, :, pl.ds(pl.multiple_of((r * n_dap + p) * CHUNK, CHUNK), CHUNK), :],
                    xr.at[:, pl.ds(pl.multiple_of(me * pitch + r * CHUNK, 8), CHUNK), :])

        pltpu.make_async_copy(*slots(my_p, my_q), xrecv_sem.at[r]).start()

        @pl.loop(1, n_all)
        def _(off):
            peer = lax.rem(me + off, n_all)
            src, dst = slots(peer // n_dap2, lax.rem(peer, n_dap2))
            pltpu.make_async_remote_copy(src_ref=src, dst_ref=dst, send_sem=xsend_sem.at[r], recv_sem=xrecv_sem.at[r],
                                         device_id=coords(peer), device_id_type=MESH).start()

    def contract_chunk(r, q, blocks):
        for t, tile in enumerate(pack_tiles(blocks, cols)):
            xs[q, t, pl.ds(pl.multiple_of(r * n_dap * CHUNK, CHUNK), n_dap * CHUNK), :] = tile

    def gather_rows(ref, r):
        return jnp.concatenate([ref[chunk_rows(p, r), :] for p in range(n_dap)], axis=0)

    def contract_outgoing(parity):
        @pl.loop(0, n_chunks)
        def _(r):
            lane = lax.rem(lane_iota((n_dap * CHUNK, n_dap2 * LANES)), LANES)
            a_tiles = [gather_rows(recv.at[parity, 0, t], r) for t in range(TILES)]
            zero = jnp.zeros_like(a_tiles[0])
            low = [jnp.where(lane < cols, a, zero) for a in a_tiles]
            high = [jnp.where(lane < cols, zero, a) for a in a_tiles]

            @pl.loop(0, n_dap2)
            def _(q):
                b_tiles = [recv[parity, 1, t, pl.ds(pl.multiple_of(q * cols, 16), cols), :] for t in range(TILES)]

                def dot(a, b):
                    x = lax.dot_general(a, b, (((1,), (1,)), ((), ())), preferred_element_type=jnp.float32)
                    return jnp.concatenate([x, jnp.zeros((x.shape[0], LANES - cols), jnp.float32)], axis=1)

                blocks = [dot(low[t], b_tiles[t]) for t in range(TILES)]
                blocks.append(dot(high[0], b_tiles[0]) + dot(high[1], b_tiles[1]) + dot(high[2], b_tiles[2]))
                contract_chunk(r, q, blocks)

            send_x(r)

    def contract_incoming(parity):
        @pl.loop(0, n_dap2)
        def _(q):
            lanes = pl.ds(pl.multiple_of(q * LANES, LANES), LANES)
            for side in range(2):
                tiles = [recv[parity, side, t, :, lanes] for t in range(TILES)]
                last = last_group([tile.astype(jnp.float32) for tile in tiles], cols).astype(jnp.bfloat16)
                if side:
                    bl[:, lanes] = last
                else:
                    for g, tile in enumerate([*tiles, last]):
                        at[g, pl.ds(pl.multiple_of(q * cols, 16), cols), :] = tile.T[:cols]

        @pl.loop(0, n_chunks)
        def _(r):
            a_all = [gather_rows(at.at[g], r) for g in range(GROUPS)]

            @pl.loop(0, n_dap2)
            def _(q):
                lanes = pl.ds(pl.multiple_of(q * LANES, LANES), LANES)
                b_all = [*[recv[parity, 1, t, :, lanes] for t in range(TILES)], bl[:, lanes]]
                contract_chunk(r, q, [jnp.dot(a, b, preferred_element_type=jnp.float32) for a, b in zip(a_all, b_all)])

            send_x(r)

    def exchange(update, parity, contract, more):
        for r in range(n_chunks):
            wait_bytes(recv.at[parity, :, :, pl.ds(0, n_dap * CHUNK), :], recv_sem.at[parity, r])
        contract(parity)
        for r in range(n_chunks):
            wait_bytes(send.at[r, pl.ds(0, n_all - 1)], send_sem.at[r])
        load_params(2, update)

        def arrived(r):
            wait_bytes(xs.at[:, :, pl.ds(0, n_dap * CHUNK), :], xrecv_sem.at[r])

        def go_on():
            load_params(0, update + 1)

            @pl.loop(0, n_chunks)
            def _(r):
                arrived(r)

                def body(indices, local):
                    states = finish_rows(indices, update)
                    for i, state in zip(indices, states):
                        zt[i] = state
                    project_rows(indices, local, states, update + 1)

                for_rows(r, body)
                send_chunk(r, 1 - parity)

        def end():
            @pl.loop(0, n_chunks)
            def _(r):
                arrived(r)

                def body(indices, local):
                    for i, state in zip(indices, finish_rows(indices, update)):
                        out_ref[i] = state.T[:cols]

                for_rows(r, body)

        if more is None:
            go_on()
        else:
            pl.when(more)(go_on)
            pl.when(jnp.logical_not(more))(end)
        for r in range(n_chunks):
            wait_bytes(xr.at[:, pl.ds(0, (n_all - 1) * CHUNK), :], xsend_sem.at[r])

    load_params(0, 0)
    pl.semaphore_wait(barrier, n_all - 1)

    @pl.loop(0, n_chunks)
    def _(r):
        def body(indices, local):
            states = [jnp.concatenate([z_ref[i].T, jnp.zeros((width, LANES - cols), jnp.float32)], axis=1) for i in indices]
            for i, state in zip(indices, states):
                zt[i] = state
            project_rows(indices, local, states, 0)

        for_rows(r, body)
        send_chunk(r, 0)

    @pl.loop(0, n_updates // 2)
    def _(layer):
        exchange(2 * layer, 0, contract_outgoing, None)
        exchange(2 * layer + 1, 1, contract_incoming, layer < n_updates // 2 - 1)


def solution(mesh):
    n_dap, n_dap2 = mesh.shape["dap"], mesh.shape["dap2"]
    n_all = n_dap * n_dap2
    pair_spec = P(("data", "dap"), "dap2", None)
    mask_spec = P(("data", "dap"), "dap2")

    def local_stack(pair_act, pair_mask, ln_z, w_ab, w_g, ln_x, w_o):
        rows, cols, width = pair_act.shape
        n_updates = w_o.shape[0] * w_o.shape[1]
        per = width // GROUPS
        full = rows * n_dap
        pitch, stage_pitch = rows + 8, CHUNK + 8
        n_chunks = rows // CHUNK
        mask = jnp.pad(pair_mask.astype(jnp.float32), ((0, 0), (0, LANES - cols)))
        w_ab = w_ab.reshape(n_updates, width, 4, GROUPS, per).transpose(0, 3, 2, 4, 1).reshape(n_updates, 4 * width, width)
        w_g = w_g.reshape(n_updates, width, width).transpose(0, 2, 1)
        w_o = w_o.reshape(n_updates, width, width).transpose(0, 2, 1)
        weights = jnp.concatenate([w_ab, w_g, w_o], axis=1)
        norms = jnp.concatenate([ln_z, ln_x], axis=2).reshape(n_updates, 4, width).transpose(0, 2, 1).astype(jnp.float32)
        vmem = pl.BlockSpec(memory_space=pltpu.VMEM)
        return pl.pallas_call(
            functools.partial(kernel, n_dap, n_dap2, n_updates),
            out_shape=jax.ShapeDtypeStruct((rows, cols, width), jnp.float32),
            in_specs=[vmem] * 4,
            out_specs=vmem,
            scratch_shapes=[
                pltpu.VMEM((rows, width, LANES), jnp.float32),
                pltpu.VMEM((rows, width, LANES), jnp.bfloat16),
                pltpu.VMEM((2, TILES, n_all * stage_pitch, LANES), jnp.float32),
                pltpu.VMEM((n_chunks, n_all, 2, TILES, CHUNK, LANES), jnp.bfloat16),
                pltpu.VMEM((2, 2, TILES, full, n_dap2 * LANES), jnp.bfloat16),
                pltpu.VMEM((GROUPS, full, full), jnp.bfloat16),
                pltpu.VMEM((full, n_dap2 * LANES), jnp.bfloat16),
                pltpu.VMEM((n_dap2, TILES, full, LANES), jnp.float32),
                pltpu.VMEM((TILES, n_all * pitch, LANES), jnp.float32),
                pltpu.VMEM((4, width, LANES), jnp.float32),
                pltpu.SemaphoreType.DMA((n_chunks,)),
                pltpu.SemaphoreType.DMA((2, n_chunks)),
                pltpu.SemaphoreType.DMA((n_chunks,)),
                pltpu.SemaphoreType.DMA((n_chunks,)),
            ],
            compiler_params=pltpu.CompilerParams(collective_id=0, has_side_effects=True, vmem_limit_bytes=60 * 1024 * 1024),
            name="triangle_stack",
        )(pair_act, mask, weights, norms)

    return jax.shard_map(local_stack, mesh=mesh, in_specs=(pair_spec, mask_spec, P(), P(), P(), P(), P()), out_specs=pair_spec, check_vma=False)
```

time: 802 us -> 504 us (0.63)
  Pallas kernels: 791 us -> 493 us
    pallas_call x1, Pallas kernels: 791 us -> 493 us  [local_stack(): pl.pallas_call(functools.partial(kernel, n_dap, n_dap2, n_updates), out_s...]
where the time goes in v2:
time: 504 us; the launch traced here: 503 us
  Pallas kernels  493 us (98%)
  local copies, waits for them, and re-layouts  7.9 us (2%)
    pallas_call x1, Pallas kernels, local_stack(): pl.pallas_call(functools.partial(kernel, n_dap, n_dap2, n_updates), out_s...  493 us

profile of v2, /device:TPU:97, one launch (start us, length us, event | category | flops | bytes accessed | tf_op | source)
XLA Modules:
  0.0 503.5 jit_solution(4501182510175519672)
XLA Ops:
  0.0 0.0 copy-start
  0.0 0.8 maximum_convert_fusion
  0.8 0.7 convert_element_type.12
  1.6 0.6 pad.4.m_ref
  2.2 1.1 copy.14
  3.3 1.1 copy.15
  4.4 1.1 copy.16
  5.5 0.0 copy-done
  5.5 0.7 copy.12
  6.1 0.1 copy.13
  6.3 1.3 pad_maximum_fusion.w_ref
  7.5 492.7 %triangle_stack.1 = f32[48,96,128]{2,1,0:T(8,128)} custom-call(f32[48,96,128]{2,1,0:T(8,128)} %z_ref.1, f32[48,128]{1,0:T(8,128)} %pad.4.m_ref, bf16[8,768,128]{2,1,0:T(8,128)(2,1)} %pad_maximum_fusion.w_ref, f32[8,128,4]{2,1,0:T(8,128)} %bitcast.15), custom_call_target="tpu_custom_call" | custom-call | tf_op jit(solution)/shard_map/triangle_stack/pallas_call | solution.py:276
  500.2 3.2 copy.18
Async XLA Ops:
  0.0 5.5 %copy-start = (bf16[4,2,128,512]{3,2,1,0:T(8,128)(2,1)S(1)}, bf16[4,2,128,512]{3,2,1,0:T(8,128)(2,1)}, u32[]{:S(2)}) copy-start(bf16[4,2,128,512]{3,2,1,0:T(8,128)(2,1)} %param.10) | copy-start | bytes 3145732

commit v3 on v2

--- a/solution.py
+++ b/solution.py
@@ -33,6 +33,19 @@
     return jnp.where(lane < part, moved[0], jnp.where(lane < 2 * part, moved[1], moved[2]))
 
 
+def pack_columns(blocks, cols):
+    part = LANES - cols
+    lane = lane_iota(blocks[0].shape)
+    tiles = []
+    for t in range(TILES):
+        moved = [block if g == t else pltpu.roll(block, part * (g - t) % LANES, 1) for g, block in enumerate(blocks)]
+        tile = moved[GROUPS - 1]
+        for g in reversed(range(GROUPS - 1)):
+            tile = jnp.where(lane < part * (g + 1), moved[g], tile)
+        tiles.append(tile)
+    return tiles
+
+
 def norm_sublanes(values, gain, bias):
     mean = jnp.mean(values, axis=0, keepdims=True)
     centered = values - mean
@@ -40,14 +53,15 @@
     return (centered * lax.rsqrt(variance + LN_EPS) * gain + bias).astype(jnp.bfloat16)
 
 
-def kernel(n_dap, n_dap2, n_updates, z_ref, m_ref, w_ref, ln_ref, out_ref, zt, zn, stage, send, recv, at, bl, xs, xr, lnb,
+def kernel(n_dap, n_dap2, n_updates, z_ref, m_ref, w_ref, ln_ref, out_ref, zt, zn, stage, send, recv, bl, xs, xr, lnb,
            send_sem, recv_sem, xsend_sem, xrecv_sem):
     rows, cols, width = z_ref.shape
     n_all = n_dap * n_dap2
-    pitch, stage_pitch = xr.shape[1] // n_all, stage.shape[2] // n_all
+    pitch, stage_pitch = xr.shape[1] // n_all, stage.shape[1] // n_all
     per = width // GROUPS
     full = rows * n_dap
     n_chunks = rows // CHUNK
+    halves = cols // rows
     my_p, my_q = lax.axis_index("dap"), lax.axis_index("dap2")
     me = my_p * n_dap2 + my_q
 
@@ -62,7 +76,7 @@
         for k in (first, first + 1):
             lnb[k] = jnp.broadcast_to(ln_ref[update, :, k:k + 1], (width, LANES))
 
-    def project_rows(indices, local, states, update):
+    def project_rows(indices, local, states, update, incoming):
         normed = [norm_sublanes(state, lnb[0], lnb[1]) for state in states]
         for i, n_row in zip(indices, normed):
             zn[i] = n_row
@@ -75,9 +89,9 @@
                 a_blocks.append(jax.nn.sigmoid(q[per:2 * per]) * q[:per] * keep)
                 b_blocks.append(jax.nn.sigmoid(q[3 * per:]) * q[2 * per:3 * per] * keep)
         for k, sides in zip(local, blocks):
-            for side in range(2):
-                for t, tile in enumerate(pack_tiles(sides[side], cols)):
-                    stage[side, t, pl.ds(k, n_all, stride=stage_pitch), :] = tile
+            a_pack = pack_columns if incoming else pack_tiles
+            for t, tile in enumerate([*pack_tiles(sides[1], cols), *a_pack(sides[0], cols)]):
+                stage[t, pl.ds(k, n_all, stride=stage_pitch), :] = tile
 
     def finish_rows(indices, update):
         tiles = [[xr[t, pl.ds(i, n_all, stride=pitch), :] for t in range(TILES)] for i in indices]
@@ -102,21 +116,50 @@
     def wait_bytes(ref, sem):
         pltpu.make_async_copy(ref, ref, sem).wait()
 
-    def send_chunk(r, parity):
-        @pl.loop(0, n_all)
-        def _(g):
-            for side in range(2):
-                for t in range(TILES):
-                    send[r, g, side, t] = stage[side, t, pl.ds(pl.multiple_of(g * stage_pitch, 8), CHUNK), :].astype(jnp.bfloat16)
-
-        slot = recv.at[parity, :, :, chunk_rows(my_p, r), pl.ds(pl.multiple_of(my_q * LANES, LANES), LANES)]
-        pltpu.make_async_copy(send.at[r, me], slot, recv_sem.at[parity, r]).start()
+    def first_tiles(parity):
+        return TILES + parity
+
+    def send_part(parity, part, tiles, first_row, n_rows):
+        row = pl.multiple_of(my_p * rows + first_row, CHUNK)
+        slot = recv.at[parity, tiles, pl.ds(row, n_rows), pl.ds(pl.multiple_of(my_q * LANES, LANES), LANES)]
+        here = pl.ds(pl.multiple_of(first_row, CHUNK), n_rows)
+        pltpu.make_async_copy(send.at[me, tiles, here], slot, recv_sem.at[parity, part]).start()
 
         @pl.loop(1, n_all)
         def _(off):
             peer = lax.rem(me + off, n_all)
-            pltpu.make_async_remote_copy(src_ref=send.at[r, peer], dst_ref=slot, send_sem=send_sem.at[r], recv_sem=recv_sem.at[parity, r],
-                                         device_id=coords(peer), device_id_type=MESH).start()
+            pltpu.make_async_remote_copy(src_ref=send.at[peer, tiles, here], dst_ref=slot, send_sem=send_sem.at[part],
+                                         recv_sem=recv_sem.at[parity, part], device_id=coords(peer), device_id_type=MESH).start()
+
+    def pack_chunk(r):
+        @pl.loop(0, n_all)
+        def _(g):
+            for t in range(2 * TILES):
+                send[g, t, pl.ds(pl.multiple_of(r * CHUNK, CHUNK), CHUNK)] = stage[t, pl.ds(pl.multiple_of(g * stage_pitch, 8), CHUNK), :].astype(jnp.bfloat16)
+
+    def send_chunk(r, parity):
+        pack_chunk(r)
+        if r == 0:
+            send_part(parity, 0, pl.ds(0, 2 * TILES), 0, CHUNK)
+        else:
+            send_part(parity, r, pl.ds(0, first_tiles(parity)), r * CHUNK, CHUNK)
+        if r == n_chunks - 1:
+            send_part(parity, n_chunks, pl.ds(first_tiles(parity), 2 * TILES - first_tiles(parity)), CHUNK, rows - CHUNK)
+
+    def part_shape(parity, part):
+        if part == 0:
+            return 2 * TILES, CHUNK
+        if part < n_chunks:
+            return first_tiles(parity), CHUNK
+        return 2 * TILES - first_tiles(parity), rows - CHUNK
+
+    def wait_received(parity, part):
+        tiles, n_rows = part_shape(parity, part)
+        wait_bytes(recv.at[parity, pl.ds(0, tiles), pl.ds(0, n_dap * n_rows), :], recv_sem.at[parity, part])
+
+    def wait_sent(parity, part):
+        tiles, n_rows = part_shape(parity, part)
+        wait_bytes(send.at[pl.ds(0, n_all - 1), pl.ds(0, tiles), pl.ds(0, n_rows)], send_sem.at[part])
 
     def send_x(r):
         def slots(p, q):
@@ -140,17 +183,17 @@
         return jnp.concatenate([ref[chunk_rows(p, r), :] for p in range(n_dap)], axis=0)
 
     def contract_outgoing(parity):
-        @pl.loop(0, n_chunks)
-        def _(r):
+        def chunk(r):
             lane = lax.rem(lane_iota((n_dap * CHUNK, n_dap2 * LANES)), LANES)
-            a_tiles = [gather_rows(recv.at[parity, 0, t], r) for t in range(TILES)]
+            a_tiles = [gather_rows(recv.at[parity, TILES + t], r) for t in range(TILES)]
             zero = jnp.zeros_like(a_tiles[0])
             low = [jnp.where(lane < cols, a, zero) for a in a_tiles]
             high = [jnp.where(lane < cols, zero, a) for a in a_tiles]
 
             @pl.loop(0, n_dap2)
             def _(q):
-                b_tiles = [recv[parity, 1, t, pl.ds(pl.multiple_of(q * cols, 16), cols), :] for t in range(TILES)]
+                b_tiles = [jnp.concatenate([recv[parity, t, chunk_rows(q * halves + h, s), :] for s in range(n_chunks) for h in range(halves)], axis=0)
+                           for t in range(TILES)]
 
                 def dot(a, b):
                     x = lax.dot_general(a, b, (((1,), (1,)), ((), ())), preferred_element_type=jnp.float32)
@@ -162,37 +205,45 @@
 
             send_x(r)
 
+        for r in range(n_chunks):
+            wait_received(parity, r)
+        chunk(0)
+        wait_received(parity, n_chunks)
+        pl.loop(1, n_chunks)(chunk)
+
     def contract_incoming(parity):
-        @pl.loop(0, n_dap2)
-        def _(q):
-            lanes = pl.ds(pl.multiple_of(q * LANES, LANES), LANES)
-            for side in range(2):
-                tiles = [recv[parity, side, t, :, lanes] for t in range(TILES)]
-                last = last_group([tile.astype(jnp.float32) for tile in tiles], cols).astype(jnp.bfloat16)
-                if side:
-                    bl[:, lanes] = last
-                else:
-                    for g, tile in enumerate([*tiles, last]):
-                        at[g, pl.ds(pl.multiple_of(q * cols, 16), cols), :] = tile.T[:cols]
-
-        @pl.loop(0, n_chunks)
-        def _(r):
-            a_all = [gather_rows(at.at[g], r) for g in range(GROUPS)]
+        def chunk(r):
+            part = LANES - cols
+            turned = [recv[parity, TILES + r, :, q * LANES:(q + 1) * LANES].T for q in range(n_dap2)]
+            a_all = [jnp.concatenate([a[g * part:(g + 1) * part] for a in turned], axis=0) for g in range(GROUPS)]
 
             @pl.loop(0, n_dap2)
             def _(q):
                 lanes = pl.ds(pl.multiple_of(q * LANES, LANES), LANES)
-                b_all = [*[recv[parity, 1, t, :, lanes] for t in range(TILES)], bl[:, lanes]]
+                b_all = [*[recv[parity, t, :, lanes] for t in range(TILES)], bl[:, lanes]]
                 contract_chunk(r, q, [jnp.dot(a, b, preferred_element_type=jnp.float32) for a, b in zip(a_all, b_all)])
 
             send_x(r)
 
+        for r in range(n_chunks):
+            wait_received(parity, r)
+
+            @pl.loop(0, n_dap)
+            def _(p):
+                here = chunk_rows(p, r)
+                for q in range(n_dap2):
+                    lanes = slice(q * LANES, (q + 1) * LANES)
+                    tiles = [recv[parity, t, here, lanes].astype(jnp.float32) for t in range(TILES)]
+                    bl[here, lanes] = last_group(tiles, cols).astype(jnp.bfloat16)
+
+        chunk(0)
+        wait_received(parity, n_chunks)
+        pl.loop(1, n_chunks)(chunk)
+
     def exchange(update, parity, contract, more):
-        for r in range(n_chunks):
-            wait_bytes(recv.at[parity, :, :, pl.ds(0, n_dap * CHUNK), :], recv_sem.at[parity, r])
         contract(parity)
-        for r in range(n_chunks):
-            wait_bytes(send.at[r, pl.ds(0, n_all - 1)], send_sem.at[r])
+        for part in range(n_chunks + 1):
+            wait_sent(parity, part)
         load_params(2, update)
 
         def arrived(r):
@@ -201,16 +252,14 @@
         def go_on():
             load_params(0, update + 1)
 
-            @pl.loop(0, n_chunks)
-            def _(r):
+            def body(indices, local):
+                states = finish_rows(indices, update)
+                for i, state in zip(indices, states):
+                    zt[i] = state
+                project_rows(indices, local, states, update + 1, incoming=parity == 0)
+
+            for r in range(n_chunks):
                 arrived(r)
-
-                def body(indices, local):
-                    states = finish_rows(indices, update)
-                    for i, state in zip(indices, states):
-                        zt[i] = state
-                    project_rows(indices, local, states, update + 1)
-
                 for_rows(r, body)
                 send_chunk(r, 1 - parity)
 
@@ -221,7 +270,11 @@
 
                 def body(indices, local):
                     for i, state in zip(indices, finish_rows(indices, update)):
-                        out_ref[i] = state.T[:cols]
+                        turned = state.T
+                        for s in range(n_chunks):
+                            for h in range(halves):
+                                lane = (s * halves + h) * CHUNK
+                                out_ref[i, h * rows + s * CHUNK:h * rows + (s + 1) * CHUNK, :] = turned[lane:lane + CHUNK]
 
                 for_rows(r, body)
 
@@ -236,15 +289,18 @@
     load_params(0, 0)
     pl.semaphore_wait(barrier, n_all - 1)
 
-    @pl.loop(0, n_chunks)
-    def _(r):
-        def body(indices, local):
-            states = [jnp.concatenate([z_ref[i].T, jnp.zeros((width, LANES - cols), jnp.float32)], axis=1) for i in indices]
-            for i, state in zip(indices, states):
-                zt[i] = state
-            project_rows(indices, local, states, 0)
-
-        for_rows(r, body)
+    def first(indices, local):
+        def turn(i):
+            order = [z_ref[i, h * rows + s * CHUNK:h * rows + (s + 1) * CHUNK, :] for s in range(n_chunks) for h in range(halves)]
+            return jnp.concatenate([jnp.concatenate(order, axis=0).T, jnp.zeros((width, LANES - cols), jnp.float32)], axis=1)
+
+        states = [turn(i) for i in indices]
+        for i, state in zip(indices, states):
+            zt[i] = state
+        project_rows(indices, local, states, 0, incoming=False)
+
+    for r in range(n_chunks):
+        for_rows(r, first)
         send_chunk(r, 0)
 
     @pl.loop(0, n_updates // 2)
@@ -266,7 +322,8 @@
         full = rows * n_dap
         pitch, stage_pitch = rows + 8, CHUNK + 8
         n_chunks = rows // CHUNK
-        mask = jnp.pad(pair_mask.astype(jnp.float32), ((0, 0), (0, LANES - cols)))
+        mask = pair_mask.astype(jnp.float32).reshape(rows, cols // rows, rows // CHUNK, CHUNK).transpose(0, 2, 1, 3).reshape(rows, cols)
+        mask = jnp.pad(mask, ((0, 0), (0, LANES - cols)))
         w_ab = w_ab.reshape(n_updates, width, 4, GROUPS, per).transpose(0, 3, 2, 4, 1).reshape(n_updates, 4 * width, width)
         w_g = w_g.reshape(n_updates, width, width).transpose(0, 2, 1)
         w_o = w_o.reshape(n_updates, width, width).transpose(0, 2, 1)
@@ -281,16 +338,15 @@
             scratch_shapes=[
                 pltpu.VMEM((rows, width, LANES), jnp.float32),
                 pltpu.VMEM((rows, width, LANES), jnp.bfloat16),
-                pltpu.VMEM((2, TILES, n_all * stage_pitch, LANES), jnp.float32),
-                pltpu.VMEM((n_chunks, n_all, 2, TILES, CHUNK, LANES), jnp.bfloat16),
-                pltpu.VMEM((2, 2, TILES, full, n_dap2 * LANES), jnp.bfloat16),
-                pltpu.VMEM((GROUPS, full, full), jnp.bfloat16),
+                pltpu.VMEM((2 * TILES, n_all * stage_pitch, LANES), jnp.float32),
+                pltpu.VMEM((n_all, 2 * TILES, rows, LANES), jnp.bfloat16),
+                pltpu.VMEM((2, 2 * TILES, full, n_dap2 * LANES), jnp.bfloat16),
                 pltpu.VMEM((full, n_dap2 * LANES), jnp.bfloat16),
                 pltpu.VMEM((n_dap2, TILES, full, LANES), jnp.float32),
                 pltpu.VMEM((TILES, n_all * pitch, LANES), jnp.float32),
                 pltpu.VMEM((4, width, LANES), jnp.float32),
-                pltpu.SemaphoreType.DMA((n_chunks,)),
-                pltpu.SemaphoreType.DMA((2, n_chunks)),
+                pltpu.SemaphoreType.DMA((n_chunks + 1,)),
+                pltpu.SemaphoreType.DMA((2, n_chunks + 1)),
                 pltpu.SemaphoreType.DMA((n_chunks,)),
                 pltpu.SemaphoreType.DMA((n_chunks,)),
             ],

time: 504 us -> 474 us (0.940)
  Pallas kernels: 493 us -> 463 us
    pallas_call x1, Pallas kernels: 493 us -> 463 us  [local_stack(): pl.pallas_call(functools.partial(kernel, n_dap, n_dap2, n_updates), out_s...]
where the time goes in v3:
time: 474 us
  Pallas kernels  463 us (98%)
  local copies, waits for them, and re-layouts  8.81 us (2%)
    pallas_call x1, Pallas kernels, local_stack(): pl.pallas_call(functools.partial(kernel, n_dap, n_dap2, n_updates), out_s...  463 us

profile of v3, /device:TPU:97, one launch (start us, length us, event | category | flops | bytes accessed | tf_op | source)
XLA Modules:
  0.0 474.0 jit_solution(15000356018516233376)
XLA Ops:
  0.0 0.0 copy-start
  0.0 0.8 maximum_convert_fusion
  0.8 0.8 copy.13
  1.7 0.1 copy.15
  1.7 0.6 pad.4.m_ref
  2.4 1.1 copy.18
  3.5 1.1 copy.19
  4.6 1.1 copy.20
  5.7 0.0 copy-done
  5.7 0.7 copy.16
  6.3 0.1 copy.17
  6.4 1.3 pad_maximum_fusion.w_ref
  7.7 463.1 %triangle_stack.1 = f32[48,96,128]{2,1,0:T(8,128)} custom-call(f32[48,96,128]{2,1,0:T(8,128)} %z_ref.1, f32[48,128]{1,0:T(8,128)} %pad.4.m_ref, bf16[8,768,128]{2,1,0:T(8,128)(2,1)} %pad_maximum_fusion.w_ref, f32[8,128,4]{2,1,0:T(8,128)} %bitcast.19), custom_call_target="tpu_custom_call" | custom-call | tf_op jit(solution)/shard_map/triangle_stack/pallas_call | solution.py:333
  470.8 3.2 copy.22
  (2 shorter events, 0.0 us)
Async XLA Ops:
  0.0 5.7 %copy-start = (bf16[4,2,128,512]{3,2,1,0:T(8,128)(2,1)S(1)}, bf16[4,2,128,512]{3,2,1,0:T(8,128)(2,1)}, u32[]{:S(2)}) copy-start(bf16[4,2,128,512]{3,2,1,0:T(8,128)(2,1)} %param.10) | copy-start | bytes 3145732

commit v4 on v3

--- a/solution.py
+++ b/solution.py
@@ -12,7 +12,7 @@
 GROUPS = 4
 TILES = 3
 CHUNK = 16
-UNROLL = 2
+UNROLL = 8
 MESH = pl.DeviceIdType.MESH
 
 
@@ -107,8 +107,22 @@
             local = [k * UNROLL + s for s in range(UNROLL)]
             body([r * CHUNK + i for i in local], local)
 
-    def coords(peer):
-        return {"dap": peer // n_dap2, "dap2": lax.rem(peer, n_dap2)}
+    def to_others(send_to):
+        def row_of(step, columns):
+            p = lax.rem(my_p + step, n_dap)
+            for column in columns:
+                send_to(p, lax.rem(my_q + column, n_dap2))
+
+        far = sorted(range(n_dap2), key=lambda column: -min(column, n_dap2 - column))
+        row_of(n_dap // 2, far)
+
+        @pl.loop(1, n_dap // 2)
+        def _(k):
+            for column in far:
+                row_of(n_dap // 2 - k, (column,))
+                row_of(n_dap // 2 + k, (column,))
+
+        row_of(0, far[:-1])
 
     def chunk_rows(p, r):
         return pl.ds(pl.multiple_of(p * rows + r * CHUNK, CHUNK), CHUNK)
@@ -125,11 +139,11 @@
         here = pl.ds(pl.multiple_of(first_row, CHUNK), n_rows)
         pltpu.make_async_copy(send.at[me, tiles, here], slot, recv_sem.at[parity, part]).start()
 
-        @pl.loop(1, n_all)
-        def _(off):
-            peer = lax.rem(me + off, n_all)
-            pltpu.make_async_remote_copy(src_ref=send.at[peer, tiles, here], dst_ref=slot, send_sem=send_sem.at[part],
-                                         recv_sem=recv_sem.at[parity, part], device_id=coords(peer), device_id_type=MESH).start()
+        def send_to(p, q):
+            pltpu.make_async_remote_copy(src_ref=send.at[p * n_dap2 + q, tiles, here], dst_ref=slot, send_sem=send_sem.at[part],
+                                         recv_sem=recv_sem.at[parity, part], device_id={"dap": p, "dap2": q}, device_id_type=MESH).start()
+
+        to_others(send_to)
 
     def pack_chunk(r):
         @pl.loop(0, n_all)
@@ -168,16 +182,18 @@
 
         pltpu.make_async_copy(*slots(my_p, my_q), xrecv_sem.at[r]).start()
 
-        @pl.loop(1, n_all)
-        def _(off):
-            peer = lax.rem(me + off, n_all)
-            src, dst = slots(peer // n_dap2, lax.rem(peer, n_dap2))
+        def send_to(p, q):
+            src, dst = slots(p, q)
             pltpu.make_async_remote_copy(src_ref=src, dst_ref=dst, send_sem=xsend_sem.at[r], recv_sem=xrecv_sem.at[r],
-                                         device_id=coords(peer), device_id_type=MESH).start()
-
-    def contract_chunk(r, q, blocks):
-        for t, tile in enumerate(pack_tiles(blocks, cols)):
-            xs[q, t, pl.ds(pl.multiple_of(r * n_dap * CHUNK, CHUNK), n_dap * CHUNK), :] = tile
+                                         device_id={"dap": p, "dap2": q}, device_id_type=MESH).start()
+
+        to_others(send_to)
+
+    def contract_chunk(r, pair, blocks):
+        for k in range(2):
+            halved = [block[:, k * LANES:(k + 1) * LANES] for block in blocks]
+            for t, tile in enumerate(pack_tiles(halved, cols)):
+                xs[2 * pair + k, t, pl.ds(pl.multiple_of(r * n_dap * CHUNK, CHUNK), n_dap * CHUNK), :] = tile
 
     def gather_rows(ref, r):
         return jnp.concatenate([ref[chunk_rows(p, r), :] for p in range(n_dap)], axis=0)
@@ -190,18 +206,22 @@
             low = [jnp.where(lane < cols, a, zero) for a in a_tiles]
             high = [jnp.where(lane < cols, zero, a) for a in a_tiles]
 
-            @pl.loop(0, n_dap2)
-            def _(q):
-                b_tiles = [jnp.concatenate([recv[parity, t, chunk_rows(q * halves + h, s), :] for s in range(n_chunks) for h in range(halves)], axis=0)
-                           for t in range(TILES)]
+            @pl.loop(0, n_dap2 // 2)
+            def _(pair):
+                def b_rows(t):
+                    pieces = []
+                    for k in range(2):
+                        pieces += [recv[parity, t, chunk_rows((2 * pair + k) * halves + h, s), :] for s in range(n_chunks) for h in range(halves)]
+                        pieces.append(jnp.zeros((LANES - cols, n_dap2 * LANES), jnp.bfloat16))
+                    return jnp.concatenate(pieces, axis=0)
 
                 def dot(a, b):
-                    x = lax.dot_general(a, b, (((1,), (1,)), ((), ())), preferred_element_type=jnp.float32)
-                    return jnp.concatenate([x, jnp.zeros((x.shape[0], LANES - cols), jnp.float32)], axis=1)
-
+                    return lax.dot_general(a, b, (((1,), (1,)), ((), ())), preferred_element_type=jnp.float32)
+
+                b_tiles = [b_rows(t) for t in range(TILES)]
                 blocks = [dot(low[t], b_tiles[t]) for t in range(TILES)]
                 blocks.append(dot(high[0], b_tiles[0]) + dot(high[1], b_tiles[1]) + dot(high[2], b_tiles[2]))
-                contract_chunk(r, q, blocks)
+                contract_chunk(r, pair, blocks)
 
             send_x(r)
 
@@ -217,11 +237,11 @@
             turned = [recv[parity, TILES + r, :, q * LANES:(q + 1) * LANES].T for q in range(n_dap2)]
             a_all = [jnp.concatenate([a[g * part:(g + 1) * part] for a in turned], axis=0) for g in range(GROUPS)]
 
-            @pl.loop(0, n_dap2)
-            def _(q):
-                lanes = pl.ds(pl.multiple_of(q * LANES, LANES), LANES)
+            @pl.loop(0, n_dap2 // 2)
+            def _(pair):
+                lanes = pl.ds(pl.multiple_of(pair * 2 * LANES, LANES), 2 * LANES)
                 b_all = [*[recv[parity, t, :, lanes] for t in range(TILES)], bl[:, lanes]]
-                contract_chunk(r, q, [jnp.dot(a, b, preferred_element_type=jnp.float32) for a, b in zip(a_all, b_all)])
+                contract_chunk(r, pair, [jnp.dot(a, b, preferred_element_type=jnp.float32) for a, b in zip(a_all, b_all)])
 
             send_x(r)
 

time: 474 us -> 481 us (1.015)
  Pallas kernels: 463 us -> 470 us
    pallas_call x1, Pallas kernels: 463 us -> 470 us  [local_stack(): pl.pallas_call(functools.partial(kernel, n_dap, n_dap2, n_updates), out_s...]
where the time goes in v4:
time: 481 us
  Pallas kernels  470 us (98%)
  local copies, waits for them, and re-layouts  8.81 us (2%)
    pallas_call x1, Pallas kernels, local_stack(): pl.pallas_call(functools.partial(kernel, n_dap, n_dap2, n_updates), out_s...  470 us

profile of v4, /device:TPU:97, one launch (start us, length us, event | category | flops | bytes accessed | tf_op | source)
XLA Modules:
  0.0 481.0 jit_solution(12021799491825901460)
XLA Ops:
  0.0 0.0 copy-start
  0.0 0.8 maximum_convert_fusion
  0.8 0.8 copy.13
  1.7 0.1 copy.15
  1.7 0.6 pad.4.m_ref
  2.4 1.1 copy.18
  3.5 1.1 copy.19
  4.6 1.1 copy.20
  5.7 0.0 copy-done
  5.7 0.7 copy.16
  6.3 0.1 copy.17
  6.4 1.3 pad_maximum_fusion.w_ref
  7.7 470.1 %triangle_stack.1 = f32[48,96,128]{2,1,0:T(8,128)} custom-call(f32[48,96,128]{2,1,0:T(8,128)} %z_ref.1, f32[48,128]{1,0:T(8,128)} %pad.4.m_ref, bf16[8,768,128]{2,1,0:T(8,128)(2,1)} %pad_maximum_fusion.w_ref, f32[8,128,4]{2,1,0:T(8,128)} %bitcast.19), custom_call_target="tpu_custom_call" | custom-call | tf_op jit(solution)/shard_map/triangle_stack/pallas_call | solution.py:353
  477.8 3.2 copy.22
  (2 shorter events, 0.0 us)
Async XLA Ops:
  0.0 5.7 %copy-start = (bf16[4,2,128,512]{3,2,1,0:T(8,128)(2,1)S(1)}, bf16[4,2,128,512]{3,2,1,0:T(8,128)(2,1)}, u32[]{:S(2)}) copy-start(bf16[4,2,128,512]{3,2,1,0:T(8,128)(2,1)} %param.10) | copy-start | bytes 3145732

commit v5 on v4

--- a/solution.py
+++ b/solution.py
@@ -13,6 +13,7 @@
 TILES = 3
 CHUNK = 16
 UNROLL = 8
+BATCH = 3
 MESH = pl.DeviceIdType.MESH
 
 
@@ -108,21 +109,17 @@
             body([r * CHUNK + i for i in local], local)
 
     def to_others(send_to):
-        def row_of(step, columns):
-            p = lax.rem(my_p + step, n_dap)
-            for column in columns:
-                send_to(p, lax.rem(my_q + column, n_dap2))
-
-        far = sorted(range(n_dap2), key=lambda column: -min(column, n_dap2 - column))
-        row_of(n_dap // 2, far)
-
-        @pl.loop(1, n_dap // 2)
+        def step(off):
+            peer = lax.rem(me + off, n_all)
+            send_to(lax.div(peer, n_dap2), lax.rem(peer, n_dap2))
+
+        @pl.loop(0, (n_all - 1) // BATCH)
         def _(k):
-            for column in far:
-                row_of(n_dap // 2 - k, (column,))
-                row_of(n_dap // 2 + k, (column,))
-
-        row_of(0, far[:-1])
+            for s in range(BATCH):
+                step(1 + k * BATCH + s)
+
+        for off in range((n_all - 1) // BATCH * BATCH + 1, n_all):
+            step(off)
 
     def chunk_rows(p, r):
         return pl.ds(pl.multiple_of(p * rows + r * CHUNK, CHUNK), CHUNK)
@@ -152,20 +149,22 @@
                 send[g, t, pl.ds(pl.multiple_of(r * CHUNK, CHUNK), CHUNK)] = stage[t, pl.ds(pl.multiple_of(g * stage_pitch, 8), CHUNK), :].astype(jnp.bfloat16)
 
     def send_chunk(r, parity):
+        early, late = first_tiles(parity), 2 * TILES - first_tiles(parity)
         pack_chunk(r)
-        if r == 0:
-            send_part(parity, 0, pl.ds(0, 2 * TILES), 0, CHUNK)
-        else:
-            send_part(parity, r, pl.ds(0, first_tiles(parity)), r * CHUNK, CHUNK)
-        if r == n_chunks - 1:
-            send_part(parity, n_chunks, pl.ds(first_tiles(parity), 2 * TILES - first_tiles(parity)), CHUNK, rows - CHUNK)
+        send_part(parity, r, pl.ds(0, early), r * CHUNK, CHUNK)
+
+        @pl.when(r == 0)
+        def _():
+            send_part(parity, n_chunks, pl.ds(early, late), 0, CHUNK)
+
+        @pl.when(r == n_chunks - 1)
+        def _():
+            send_part(parity, n_chunks + 1, pl.ds(early, late), CHUNK, rows - CHUNK)
 
     def part_shape(parity, part):
-        if part == 0:
-            return 2 * TILES, CHUNK
         if part < n_chunks:
             return first_tiles(parity), CHUNK
-        return 2 * TILES - first_tiles(parity), rows - CHUNK
+        return 2 * TILES - first_tiles(parity), CHUNK if part == n_chunks else rows - CHUNK
 
     def wait_received(parity, part):
         tiles, n_rows = part_shape(parity, part)
@@ -200,6 +199,10 @@
 
     def contract_outgoing(parity):
         def chunk(r):
+            @pl.when(r == 1)
+            def _():
+                wait_received(parity, n_chunks + 1)
+
             lane = lax.rem(lane_iota((n_dap * CHUNK, n_dap2 * LANES)), LANES)
             a_tiles = [gather_rows(recv.at[parity, TILES + t], r) for t in range(TILES)]
             zero = jnp.zeros_like(a_tiles[0])
@@ -225,14 +228,16 @@
 
             send_x(r)
 
-        for r in range(n_chunks):
-            wait_received(parity, r)
-        chunk(0)
-        wait_received(parity, n_chunks)
-        pl.loop(1, n_chunks)(chunk)
+        for part in range(n_chunks + 1):
+            wait_received(parity, part)
+        pl.loop(0, n_chunks)(chunk)
 
     def contract_incoming(parity):
         def chunk(r):
+            @pl.when(r == 1)
+            def _():
+                wait_received(parity, n_chunks + 1)
+
             part = LANES - cols
             turned = [recv[parity, TILES + r, :, q * LANES:(q + 1) * LANES].T for q in range(n_dap2)]
             a_all = [jnp.concatenate([a[g * part:(g + 1) * part] for a in turned], axis=0) for g in range(GROUPS)]
@@ -245,8 +250,9 @@
 
             send_x(r)
 
-        for r in range(n_chunks):
-            wait_received(parity, r)
+        @pl.loop(0, n_chunks)
+        def _(r):
+            wait_bytes(recv.at[parity, pl.ds(0, first_tiles(parity)), pl.ds(0, n_dap * CHUNK), :], recv_sem.at[parity, r])
 
             @pl.loop(0, n_dap)
             def _(p):
@@ -256,13 +262,12 @@
                     tiles = [recv[parity, t, here, lanes].astype(jnp.float32) for t in range(TILES)]
                     bl[here, lanes] = last_group(tiles, cols).astype(jnp.bfloat16)
 
-        chunk(0)
         wait_received(parity, n_chunks)
-        pl.loop(1, n_chunks)(chunk)
+        pl.loop(0, n_chunks)(chunk)
 
     def exchange(update, parity, contract, more):
         contract(parity)
-        for part in range(n_chunks + 1):
+        for part in range(n_chunks + 2):
             wait_sent(parity, part)
         load_params(2, update)
 
@@ -278,7 +283,8 @@
                     zt[i] = state
                 project_rows(indices, local, states, update + 1, incoming=parity == 0)
 
-            for r in range(n_chunks):
+            @pl.loop(0, n_chunks)
+            def _(r):
                 arrived(r)
                 for_rows(r, body)
                 send_chunk(r, 1 - parity)
@@ -319,7 +325,8 @@
             zt[i] = state
         project_rows(indices, local, states, 0, incoming=False)
 
-    for r in range(n_chunks):
+    @pl.loop(0, n_chunks)
+    def _(r):
         for_rows(r, first)
         send_chunk(r, 0)
 
@@ -365,8 +372,8 @@
                 pltpu.VMEM((n_dap2, TILES, full, LANES), jnp.float32),
                 pltpu.VMEM((TILES, n_all * pitch, LANES), jnp.float32),
                 pltpu.VMEM((4, width, LANES), jnp.float32),
-                pltpu.SemaphoreType.DMA((n_chunks + 1,)),
-                pltpu.SemaphoreType.DMA((2, n_chunks + 1)),
+                pltpu.SemaphoreType.DMA((n_chunks + 2,)),
+                pltpu.SemaphoreType.DMA((2, n_chunks + 2)),
                 pltpu.SemaphoreType.DMA((n_chunks,)),
                 pltpu.SemaphoreType.DMA((n_chunks,)),
             ],

time: 481 us -> 467 us (0.971)
  Pallas kernels: 470 us -> 456 us
    pallas_call x1, Pallas kernels: 470 us -> 456 us  [local_stack(): pl.pallas_call(functools.partial(kernel, n_dap, n_dap2, n_updates), out_s...]
where the time goes in v5:
time: 467 us
  Pallas kernels  456 us (98%)
  local copies, waits for them, and re-layouts  8.81 us (2%)
    pallas_call x1, Pallas kernels, local_stack(): pl.pallas_call(functools.partial(kernel, n_dap, n_dap2, n_updates), out_s...  456 us

profile of v5, /device:TPU:97, one launch (start us, length us, event | category | flops | bytes accessed | tf_op | source)
XLA Modules:
  0.0 467.1 jit_solution(1742140136081108089)
XLA Ops:
  0.0 0.0 copy-start
  0.0 0.8 maximum_convert_fusion
  0.8 0.8 copy.13
  1.7 0.1 copy.15
  1.7 0.6 pad.4.m_ref
  2.4 1.1 copy.18
  3.5 1.1 copy.19
  4.6 1.1 copy.20
  5.7 0.0 copy-done
  5.7 0.7 copy.16
  6.3 0.1 copy.17
  6.4 1.3 pad_maximum_fusion.w_ref
  7.7 456.2 %triangle_stack.1 = f32[48,96,128]{2,1,0:T(8,128)} custom-call(f32[48,96,128]{2,1,0:T(8,128)} %z_ref.1, f32[48,128]{1,0:T(8,128)} %pad.4.m_ref, bf16[8,768,128]{2,1,0:T(8,128)(2,1)} %pad_maximum_fusion.w_ref, f32[8,128,4]{2,1,0:T(8,128)} %bitcast.19), custom_call_target="tpu_custom_call" | custom-call | tf_op jit(solution)/shard_map/triangle_stack/pallas_call | solution.py:360
  463.9 3.2 copy.22
  (2 shorter events, 0.0 us)
Async XLA Ops:
  0.0 5.7 %copy-start = (bf16[4,2,128,512]{3,2,1,0:T(8,128)(2,1)S(1)}, bf16[4,2,128,512]{3,2,1,0:T(8,128)(2,1)}, u32[]{:S(2)}) copy-start(bf16[4,2,128,512]{3,2,1,0:T(8,128)(2,1)} %param.10) | copy-start | bytes 3145732

commit v6 on v5

--- a/solution.py
+++ b/solution.py
@@ -54,7 +54,7 @@
     return (centered * lax.rsqrt(variance + LN_EPS) * gain + bias).astype(jnp.bfloat16)
 
 
-def kernel(n_dap, n_dap2, n_updates, z_ref, m_ref, w_ref, ln_ref, out_ref, zt, zn, stage, send, recv, bl, xs, xr, lnb,
+def kernel(n_dap, n_dap2, n_updates, z_ref, mask_ref, ln_z_ref, w_ab_ref, w_g_ref, ln_x_ref, w_o_ref, out_ref, m_ref, w_ref, zt, zn, stage, send, recv, bl, xs, xr, lnb,
            send_sem, recv_sem, xsend_sem, xrecv_sem):
     rows, cols, width = z_ref.shape
     n_all = n_dap * n_dap2
@@ -73,18 +73,35 @@
         peer = lax.rem(me + off, n_all)
         pl.semaphore_signal(barrier, inc=1, device_id={"dap": peer // n_dap2, "dap2": lax.rem(peer, n_dap2)}, device_id_type=MESH)
 
-    def load_params(first, update):
-        for k in (first, first + 1):
-            lnb[k] = jnp.broadcast_to(ln_ref[update, :, k:k + 1], (width, LANES))
-
-    def project_rows(indices, local, states, update, incoming):
+    def turn_columns(values):
+        order = [values[h * rows + s * CHUNK:h * rows + (s + 1) * CHUNK] for s in range(n_chunks) for h in range(halves)]
+        return jnp.concatenate(order, axis=0)
+
+    def load_norm(first, norm_ref, update):
+        params = norm_ref[update].astype(jnp.float32)
+        for k in range(2):
+            lnb[first + k] = jnp.broadcast_to(params[k:k + 1], (LANES, width)).T
+
+    def load_projection(update):
+        load_norm(0, ln_z_ref, update)
+        for kind in range(4):
+            turned = w_ab_ref[update, :, kind * width:(kind + 1) * width].T
+            for g in range(GROUPS):
+                w_ref[g * 4 * per + kind * per:g * 4 * per + (kind + 1) * per, :] = turned[g * per:(g + 1) * per]
+
+    def load_finish(update):
+        load_norm(2, ln_x_ref, update)
+        w_ref[4 * width:5 * width, :] = w_g_ref[update].T
+        w_ref[5 * width:6 * width, :] = w_o_ref[update].T
+
+    def project_rows(indices, local, states, incoming):
         normed = [norm_sublanes(state, lnb[0], lnb[1]) for state in states]
         for i, n_row in zip(indices, normed):
             zn[i] = n_row
         keeps = [m_ref[pl.ds(i, 1), :] for i in indices]
         blocks = [([], []) for _ in indices]
         for g in range(GROUPS):
-            weight = w_ref[update, g * 4 * per:(g + 1) * 4 * per, :]
+            weight = w_ref[g * 4 * per:(g + 1) * 4 * per, :]
             for keep, n_row, (a_blocks, b_blocks) in zip(keeps, normed, blocks):
                 q = jnp.dot(weight, n_row, preferred_element_type=jnp.float32)
                 a_blocks.append(jax.nn.sigmoid(q[per:2 * per]) * q[:per] * keep)
@@ -94,12 +111,12 @@
             for t, tile in enumerate([*pack_tiles(sides[1], cols), *a_pack(sides[0], cols)]):
                 stage[t, pl.ds(k, n_all, stride=stage_pitch), :] = tile
 
-    def finish_rows(indices, update):
+    def finish_rows(indices):
         tiles = [[xr[t, pl.ds(i, n_all, stride=pitch), :] for t in range(TILES)] for i in indices]
         x_rows = [jnp.concatenate([*tile, last_group(tile, cols)], axis=0) for tile in tiles]
-        gates = [jnp.dot(w_ref[update, 4 * width:5 * width, :], zn[i], preferred_element_type=jnp.float32) for i in indices]
+        gates = [jnp.dot(w_ref[4 * width:5 * width, :], zn[i], preferred_element_type=jnp.float32) for i in indices]
         normed = [norm_sublanes(x_row, lnb[2], lnb[3]) for x_row in x_rows]
-        values = [jnp.dot(w_ref[update, 5 * width:6 * width, :], x_norm, preferred_element_type=jnp.float32) for x_norm in normed]
+        values = [jnp.dot(w_ref[5 * width:6 * width, :], x_norm, preferred_element_type=jnp.float32) for x_norm in normed]
         return [zt[i] + jax.nn.sigmoid(gate) * value for i, gate, value in zip(indices, gates, values)]
 
     def for_rows(r, body):
@@ -269,19 +286,19 @@
         contract(parity)
         for part in range(n_chunks + 2):
             wait_sent(parity, part)
-        load_params(2, update)
+        load_finish(update)
 
         def arrived(r):
             wait_bytes(xs.at[:, :, pl.ds(0, n_dap * CHUNK), :], xrecv_sem.at[r])
 
         def go_on():
-            load_params(0, update + 1)
+            load_projection(update + 1)
 
             def body(indices, local):
-                states = finish_rows(indices, update)
+                states = finish_rows(indices)
                 for i, state in zip(indices, states):
                     zt[i] = state
-                project_rows(indices, local, states, update + 1, incoming=parity == 0)
+                project_rows(indices, local, states, incoming=parity == 0)
 
             @pl.loop(0, n_chunks)
             def _(r):
@@ -295,7 +312,7 @@
                 arrived(r)
 
                 def body(indices, local):
-                    for i, state in zip(indices, finish_rows(indices, update)):
+                    for i, state in zip(indices, finish_rows(indices)):
                         turned = state.T
                         for s in range(n_chunks):
                             for h in range(halves):
@@ -312,18 +329,20 @@
         for r in range(n_chunks):
             wait_bytes(xr.at[:, pl.ds(0, (n_all - 1) * CHUNK), :], xsend_sem.at[r])
 
-    load_params(0, 0)
+    load_projection(0)
+    m_ref[...] = jnp.zeros((rows, LANES), jnp.float32)
+    m_ref[:, :cols] = turn_columns(mask_ref[...].astype(jnp.float32).T).T
+
+    @pl.loop(0, rows // UNROLL)
+    def _(k):
+        for s in range(UNROLL):
+            i = k * UNROLL + s
+            zt[i] = jnp.concatenate([turn_columns(z_ref[i]).T, jnp.zeros((width, LANES - cols), jnp.float32)], axis=1)
+
     pl.semaphore_wait(barrier, n_all - 1)
 
     def first(indices, local):
-        def turn(i):
-            order = [z_ref[i, h * rows + s * CHUNK:h * rows + (s + 1) * CHUNK, :] for s in range(n_chunks) for h in range(halves)]
-            return jnp.concatenate([jnp.concatenate(order, axis=0).T, jnp.zeros((width, LANES - cols), jnp.float32)], axis=1)
-
-        states = [turn(i) for i in indices]
-        for i, state in zip(indices, states):
-            zt[i] = state
-        project_rows(indices, local, states, 0, incoming=False)
+        project_rows(indices, local, [zt[i] for i in indices], incoming=False)
 
     @pl.loop(0, n_chunks)
     def _(r):
@@ -345,24 +364,19 @@
     def local_stack(pair_act, pair_mask, ln_z, w_ab, w_g, ln_x, w_o):
         rows, cols, width = pair_act.shape
         n_updates = w_o.shape[0] * w_o.shape[1]
-        per = width // GROUPS
         full = rows * n_dap
         pitch, stage_pitch = rows + 8, CHUNK + 8
         n_chunks = rows // CHUNK
-        mask = pair_mask.astype(jnp.float32).reshape(rows, cols // rows, rows // CHUNK, CHUNK).transpose(0, 2, 1, 3).reshape(rows, cols)
-        mask = jnp.pad(mask, ((0, 0), (0, LANES - cols)))
-        w_ab = w_ab.reshape(n_updates, width, 4, GROUPS, per).transpose(0, 3, 2, 4, 1).reshape(n_updates, 4 * width, width)
-        w_g = w_g.reshape(n_updates, width, width).transpose(0, 2, 1)
-        w_o = w_o.reshape(n_updates, width, width).transpose(0, 2, 1)
-        weights = jnp.concatenate([w_ab, w_g, w_o], axis=1)
-        norms = jnp.concatenate([ln_z, ln_x], axis=2).reshape(n_updates, 4, width).transpose(0, 2, 1).astype(jnp.float32)
+        flat = [array.reshape(n_updates, *array.shape[2:]) for array in (ln_z, w_ab, w_g, ln_x, w_o)]
         vmem = pl.BlockSpec(memory_space=pltpu.VMEM)
         return pl.pallas_call(
             functools.partial(kernel, n_dap, n_dap2, n_updates),
             out_shape=jax.ShapeDtypeStruct((rows, cols, width), jnp.float32),
-            in_specs=[vmem] * 4,
+            in_specs=[vmem] * 7,
             out_specs=vmem,
             scratch_shapes=[
+                pltpu.VMEM((rows, LANES), jnp.float32),
+                pltpu.VMEM((6 * width, width), jnp.bfloat16),
                 pltpu.VMEM((rows, width, LANES), jnp.float32),
                 pltpu.VMEM((rows, width, LANES), jnp.bfloat16),
                 pltpu.VMEM((2 * TILES, n_all * stage_pitch, LANES), jnp.float32),
@@ -379,6 +393,6 @@
             ],
             compiler_params=pltpu.CompilerParams(collective_id=0, has_side_effects=True, vmem_limit_bytes=60 * 1024 * 1024),
             name="triangle_stack",
-        )(pair_act, mask, weights, norms)
+        )(pair_act, pair_mask, *flat)
 
     return jax.shard_map(local_stack, mesh=mesh, in_specs=(pair_spec, mask_spec, P(), P(), P(), P(), P()), out_specs=pair_spec, check_vma=False)

time: 467 us -> 458 us (0.981)
  local copies, waits for them, and re-layouts: 8.81 us -> 3.22 us
where the time goes in v6:
time: 458 us
  Pallas kernels  454 us (99%)
    pallas_call x1, Pallas kernels, local_stack(): pl.pallas_call(functools.partial(kernel, n_dap, n_dap2, n_updates), out_s...  454 us

profile of v6, /device:TPU:97, one launch (start us, length us, event | category | flops | bytes accessed | tf_op | source)
XLA Modules:
  0.0 457.5 jit_solution(4484192963488745428)
XLA Ops:
  0.0 454.3 %triangle_stack.1 = f32[48,96,128]{2,1,0:T(8,128)} custom-call(f32[48,96,128]{2,1,0:T(8,128)} %z_ref.1, s32[48,96]{1,0:T(8,128)} %mask_ref.1, bf16[8,2,128]{2,1,0:T(2,128)(2,1)} %bitcast.8, bf16[8,128,512]{2,1,0:T(8,128)(2,1)} %bitcast.5, bf16[8,128,128]{2,1,0:T(8,128)(2,1)} %bitcast.6, bf16[8,2,128]{2,1,0:T(2,128)(2,1)} %bitcast.9, bf16[8,128,128]{2,1,0:T(8,128)(2,1)} %bitcast.7), custom_call_target="tpu_custom_call" | custom-call | tf_op jit(solution)/shard_map/triangle_stack/pallas_call | solution.py:372
  454.3 3.2 copy.9

commit v7 on v6

--- a/solution.py
+++ b/solution.py
@@ -168,20 +168,25 @@
     def send_chunk(r, parity):
         early, late = first_tiles(parity), 2 * TILES - first_tiles(parity)
         pack_chunk(r)
-        send_part(parity, r, pl.ds(0, early), r * CHUNK, CHUNK)
 
         @pl.when(r == 0)
         def _():
-            send_part(parity, n_chunks, pl.ds(early, late), 0, CHUNK)
+            send_part(parity, 0, pl.ds(0, 2 * TILES), 0, CHUNK)
+
+        @pl.when(r > 0)
+        def _():
+            send_part(parity, r, pl.ds(0, early), r * CHUNK, CHUNK)
 
         @pl.when(r == n_chunks - 1)
         def _():
-            send_part(parity, n_chunks + 1, pl.ds(early, late), CHUNK, rows - CHUNK)
+            send_part(parity, n_chunks, pl.ds(early, late), CHUNK, rows - CHUNK)
 
     def part_shape(parity, part):
+        if part == 0:
+            return 2 * TILES, CHUNK
         if part < n_chunks:
             return first_tiles(parity), CHUNK
-        return 2 * TILES - first_tiles(parity), CHUNK if part == n_chunks else rows - CHUNK
+        return 2 * TILES - first_tiles(parity), rows - CHUNK
 
     def wait_received(parity, part):
         tiles, n_rows = part_shape(parity, part)
@@ -192,24 +197,34 @@
         wait_bytes(send.at[pl.ds(0, n_all - 1), pl.ds(0, tiles), pl.ds(0, n_rows)], send_sem.at[part])
 
     def send_x(r):
-        def slots(p, q):
-            return (xs.at[q, :, pl.ds(pl.multiple_of((r * n_dap + p) * CHUNK, CHUNK), CHUNK), :],
-                    xr.at[:, pl.ds(pl.multiple_of(me * pitch + r * CHUNK, 8), CHUNK), :])
-
-        pltpu.make_async_copy(*slots(my_p, my_q), xrecv_sem.at[r]).start()
-
-        def send_to(p, q):
-            src, dst = slots(p, q)
-            pltpu.make_async_remote_copy(src_ref=src, dst_ref=dst, send_sem=xsend_sem.at[r], recv_sem=xrecv_sem.at[r],
-                                         device_id={"dap": p, "dap2": q}, device_id_type=MESH).start()
-
-        to_others(send_to)
+        def send_rows(part, first_row, n_rows):
+            def slots(p, q):
+                return (xs.at[q, :, pl.ds(pl.multiple_of(p * rows + first_row, CHUNK), n_rows), :],
+                        xr.at[:, pl.ds(pl.multiple_of(me * pitch + first_row, 8), n_rows), :])
+
+            pltpu.make_async_copy(*slots(my_p, my_q), xrecv_sem.at[part]).start()
+
+            def send_to(p, q):
+                src, dst = slots(p, q)
+                pltpu.make_async_remote_copy(src_ref=src, dst_ref=dst, send_sem=xsend_sem.at[part], recv_sem=xrecv_sem.at[part],
+                                             device_id={"dap": p, "dap2": q}, device_id_type=MESH).start()
+
+            to_others(send_to)
+
+        @pl.when(r == 0)
+        def _():
+            send_rows(0, 0, CHUNK)
+
+        @pl.when(r == n_chunks - 1)
+        def _():
+            send_rows(1, CHUNK, rows - CHUNK)
 
     def contract_chunk(r, pair, blocks):
         for k in range(2):
             halved = [block[:, k * LANES:(k + 1) * LANES] for block in blocks]
             for t, tile in enumerate(pack_tiles(halved, cols)):
-                xs[2 * pair + k, t, pl.ds(pl.multiple_of(r * n_dap * CHUNK, CHUNK), n_dap * CHUNK), :] = tile
+                for p in range(n_dap):
+                    xs[2 * pair + k, t, chunk_rows(p, r), :] = tile[p * CHUNK:(p + 1) * CHUNK]
 
     def gather_rows(ref, r):
         return jnp.concatenate([ref[chunk_rows(p, r), :] for p in range(n_dap)], axis=0)
@@ -218,7 +233,7 @@
         def chunk(r):
             @pl.when(r == 1)
             def _():
-                wait_received(parity, n_chunks + 1)
+                wait_received(parity, n_chunks)
 
             lane = lax.rem(lane_iota((n_dap * CHUNK, n_dap2 * LANES)), LANES)
             a_tiles = [gather_rows(recv.at[parity, TILES + t], r) for t in range(TILES)]
@@ -245,7 +260,7 @@
 
             send_x(r)
 
-        for part in range(n_chunks + 1):
+        for part in range(n_chunks):
             wait_received(parity, part)
         pl.loop(0, n_chunks)(chunk)
 
@@ -253,7 +268,7 @@
         def chunk(r):
             @pl.when(r == 1)
             def _():
-                wait_received(parity, n_chunks + 1)
+                wait_received(parity, n_chunks)
 
             part = LANES - cols
             turned = [recv[parity, TILES + r, :, q * LANES:(q + 1) * LANES].T for q in range(n_dap2)]
@@ -269,27 +284,34 @@
 
         @pl.loop(0, n_chunks)
         def _(r):
-            wait_bytes(recv.at[parity, pl.ds(0, first_tiles(parity)), pl.ds(0, n_dap * CHUNK), :], recv_sem.at[parity, r])
-
-            @pl.loop(0, n_dap)
-            def _(p):
-                here = chunk_rows(p, r)
-                for q in range(n_dap2):
+            @pl.when(r == 0)
+            def _():
+                wait_received(parity, 0)
+
+            @pl.when(r > 0)
+            def _():
+                wait_bytes(recv.at[parity, pl.ds(0, first_tiles(parity)), pl.ds(0, n_dap * CHUNK), :], recv_sem.at[parity, r])
+
+            @pl.loop(0, n_dap // 2)
+            def _(k):
+                for here, q in [(chunk_rows(2 * k + h, r), q) for h in range(2) for q in range(n_dap2)]:
                     lanes = slice(q * LANES, (q + 1) * LANES)
                     tiles = [recv[parity, t, here, lanes].astype(jnp.float32) for t in range(TILES)]
                     bl[here, lanes] = last_group(tiles, cols).astype(jnp.bfloat16)
 
-        wait_received(parity, n_chunks)
         pl.loop(0, n_chunks)(chunk)
 
     def exchange(update, parity, contract, more):
         contract(parity)
-        for part in range(n_chunks + 2):
+        for part in range(n_chunks + 1):
             wait_sent(parity, part)
         load_finish(update)
 
         def arrived(r):
-            wait_bytes(xs.at[:, :, pl.ds(0, n_dap * CHUNK), :], xrecv_sem.at[r])
+            for part, n_rows in enumerate((CHUNK, rows - CHUNK)):
+                @pl.when(r == part)
+                def _():
+                    wait_bytes(xs.at[:, :, pl.ds(0, n_dap * n_rows), :], xrecv_sem.at[part])
 
         def go_on():
             load_projection(update + 1)
@@ -326,8 +348,8 @@
         else:
             pl.when(more)(go_on)
             pl.when(jnp.logical_not(more))(end)
-        for r in range(n_chunks):
-            wait_bytes(xr.at[:, pl.ds(0, (n_all - 1) * CHUNK), :], xsend_sem.at[r])
+        for part, n_rows in enumerate((CHUNK, rows - CHUNK)):
+            wait_bytes(xr.at[:, pl.ds(0, (n_all - 1) * n_rows), :], xsend_sem.at[part])
 
     load_projection(0)
     m_ref[...] = jnp.zeros((rows, LANES), jnp.float32)
@@ -386,10 +408,10 @@
                 pltpu.VMEM((n_dap2, TILES, full, LANES), jnp.float32),
                 pltpu.VMEM((TILES, n_all * pitch, LANES), jnp.float32),
                 pltpu.VMEM((4, width, LANES), jnp.float32),
-                pltpu.SemaphoreType.DMA((n_chunks + 2,)),
-                pltpu.SemaphoreType.DMA((2, n_chunks + 2)),
-                pltpu.SemaphoreType.DMA((n_chunks,)),
-                pltpu.SemaphoreType.DMA((n_chunks,)),
+                pltpu.SemaphoreType.DMA((n_chunks + 1,)),
+                pltpu.SemaphoreType.DMA((2, n_chunks + 1)),
+                pltpu.SemaphoreType.DMA((2,)),
+                pltpu.SemaphoreType.DMA((2,)),
             ],
             compiler_params=pltpu.CompilerParams(collective_id=0, has_side_effects=True, vmem_limit_bytes=60 * 1024 * 1024),
             name="triangle_stack",

time: 458 us -> 468 us (1.022)
  Pallas kernels: 454 us -> 465 us
    pallas_call x1, Pallas kernels: 454 us -> 465 us  [local_stack(): pl.pallas_call(functools.partial(kernel, n_dap, n_dap2, n_updates), out_s...]
where the time goes in v7:
time: 468 us
  Pallas kernels  465 us (99%)
    pallas_call x1, Pallas kernels, local_stack(): pl.pallas_call(functools.partial(kernel, n_dap, n_dap2, n_updates), out_s...  465 us

profile of v7, /device:TPU:97, one launch (start us, length us, event | category | flops | bytes accessed | tf_op | source)
XLA Modules:
  0.0 468.2 jit_solution(7932064475791885422)
XLA Ops:
  0.0 464.9 %triangle_stack.1 = f32[48,96,128]{2,1,0:T(8,128)} custom-call(f32[48,96,128]{2,1,0:T(8,128)} %z_ref.1, s32[48,96]{1,0:T(8,128)} %mask_ref.1, bf16[8,2,128]{2,1,0:T(2,128)(2,1)} %bitcast.8, bf16[8,128,512]{2,1,0:T(8,128)(2,1)} %bitcast.5, bf16[8,128,128]{2,1,0:T(8,128)(2,1)} %bitcast.6, bf16[8,2,128]{2,1,0:T(2,128)(2,1)} %bitcast.9, bf16[8,128,128]{2,1,0:T(8,128)(2,1)} %bitcast.7), custom_call_target="tpu_custom_call" | custom-call | tf_op jit(solution)/shard_map/triangle_stack/pallas_call | solution.py:394
  464.9 3.2 copy.9

commit v8 on v6

--- a/solution.py
+++ b/solution.py
@@ -13,7 +13,6 @@
 TILES = 3
 CHUNK = 16
 UNROLL = 8
-BATCH = 3
 MESH = pl.DeviceIdType.MESH
 
 
@@ -125,18 +124,30 @@
             local = [k * UNROLL + s for s in range(UNROLL)]
             body([r * CHUNK + i for i in local], local)
 
+    def flip(value, bits, size):
+        result, place = 0, 1
+        while place < size:
+            digit = lax.rem(lax.div(value, place), 2)
+            result += place * lax.rem(digit + lax.rem(lax.div(bits, place), 2), 2)
+            place *= 2
+        return result
+
     def to_others(send_to):
-        def step(off):
-            peer = lax.rem(me + off, n_all)
-            send_to(lax.div(peer, n_dap2), lax.rem(peer, n_dap2))
-
-        @pl.loop(0, (n_all - 1) // BATCH)
+        cores = 2
+        steps = sorted(range(n_dap // cores), key=lambda step: (step == 0, step % 2 == 0, step))
+
+        def column(k, skip):
+            q = flip(my_q, k, n_dap2)
+            for core in range(cores):
+                for step in steps:
+                    if not (skip and core == 0 and step == 0):
+                        send_to(flip(my_p, jnp.int32(step * cores + core), n_dap), q)
+
+        @pl.loop(0, n_dap2 - 1)
         def _(k):
-            for s in range(BATCH):
-                step(1 + k * BATCH + s)
-
-        for off in range((n_all - 1) // BATCH * BATCH + 1, n_all):
-            step(off)
+            column(n_dap2 - 1 - k, False)
+
+        column(jnp.int32(0), True)
 
     def chunk_rows(p, r):
         return pl.ds(pl.multiple_of(p * rows + r * CHUNK, CHUNK), CHUNK)
@@ -271,10 +282,9 @@
         def _(r):
             wait_bytes(recv.at[parity, pl.ds(0, first_tiles(parity)), pl.ds(0, n_dap * CHUNK), :], recv_sem.at[parity, r])
 
-            @pl.loop(0, n_dap)
-            def _(p):
-                here = chunk_rows(p, r)
-                for q in range(n_dap2):
+            @pl.loop(0, n_dap // 2)
+            def _(k):
+                for here, q in [(chunk_rows(2 * k + h, r), q) for h in range(2) for q in range(n_dap2)]:
                     lanes = slice(q * LANES, (q + 1) * LANES)
                     tiles = [recv[parity, t, here, lanes].astype(jnp.float32) for t in range(TILES)]
                     bl[here, lanes] = last_group(tiles, cols).astype(jnp.bfloat16)

time: 458 us -> 505 us (1.10)
  Pallas kernels: 454 us -> 502 us
    pallas_call x1, Pallas kernels: 454 us -> 502 us  [local_stack(): pl.pallas_call(functools.partial(kernel, n_dap, n_dap2, n_updates), out_s...]
where the time goes in v8:
time: 505 us
  Pallas kernels  502 us (99%)
    pallas_call x1, Pallas kernels, local_stack(): pl.pallas_call(functools.partial(kernel, n_dap, n_dap2, n_updates), out_s...  502 us

profile of v8, /device:TPU:97, one launch (start us, length us, event | category | flops | bytes accessed | tf_op | source)
XLA Modules:
  0.0 505.2 jit_solution(3429054355841004605)
XLA Ops:
  0.0 502.0 %triangle_stack.1 = f32[48,96,128]{2,1,0:T(8,128)} custom-call(f32[48,96,128]{2,1,0:T(8,128)} %z_ref.1, s32[48,96]{1,0:T(8,128)} %mask_ref.1, bf16[8,2,128]{2,1,0:T(2,128)(2,1)} %bitcast.8, bf16[8,128,512]{2,1,0:T(8,128)(2,1)} %bitcast.5, bf16[8,128,128]{2,1,0:T(8,128)(2,1)} %bitcast.6, bf16[8,2,128]{2,1,0:T(2,128)(2,1)} %bitcast.9, bf16[8,128,128]{2,1,0:T(8,128)(2,1)} %bitcast.7), custom_call_target="tpu_custom_call" | custom-call | tf_op jit(solution)/shard_map/triangle_stack/pallas_call | solution.py:382
  502.0 3.2 copy.9

commit v9 on v6

--- a/solution.py
+++ b/solution.py
@@ -1,4 +1,5 @@
 import functools
+import math
 
 import jax
 import jax.numpy as jnp
@@ -14,6 +15,7 @@
 CHUNK = 16
 UNROLL = 8
 BATCH = 3
+STRIDE = 13
 MESH = pl.DeviceIdType.MESH
 
 
@@ -126,8 +128,9 @@
             body([r * CHUNK + i for i in local], local)
 
     def to_others(send_to):
+        assert math.gcd(STRIDE, n_all) == 1
         def step(off):
-            peer = lax.rem(me + off, n_all)
+            peer = lax.rem(me + off * STRIDE, n_all)
             send_to(lax.div(peer, n_dap2), lax.rem(peer, n_dap2))
 
         @pl.loop(0, (n_all - 1) // BATCH)
@@ -271,10 +274,9 @@
         def _(r):
             wait_bytes(recv.at[parity, pl.ds(0, first_tiles(parity)), pl.ds(0, n_dap * CHUNK), :], recv_sem.at[parity, r])
 
-            @pl.loop(0, n_dap)
-            def _(p):
-                here = chunk_rows(p, r)
-                for q in range(n_dap2):
+            @pl.loop(0, n_dap // 2)
+            def _(k):
+                for here, q in [(chunk_rows(2 * k + h, r), q) for h in range(2) for q in range(n_dap2)]:
                     lanes = slice(q * LANES, (q + 1) * LANES)
                     tiles = [recv[parity, t, here, lanes].astype(jnp.float32) for t in range(TILES)]
                     bl[here, lanes] = last_group(tiles, cols).astype(jnp.bfloat16)

time: 458 us -> 464 us (1.013)
  Pallas kernels: 454 us -> 460 us
    pallas_call x1, Pallas kernels: 454 us -> 460 us  [local_stack(): pl.pallas_call(functools.partial(kernel, n_dap, n_dap2, n_updates), out_s...]
where the time goes in v9:
time: 464 us; the launch traced here: 463 us
  Pallas kernels  460 us (99%)
    pallas_call x1, Pallas kernels, local_stack(): pl.pallas_call(functools.partial(kernel, n_dap, n_dap2, n_updates), out_s...  460 us

profile of v9, /device:TPU:97, one launch (start us, length us, event | category | flops | bytes accessed | tf_op | source)
XLA Modules:
  0.0 463.5 jit_solution(4378822668071255696)
XLA Ops:
  0.0 460.2 %triangle_stack.1 = f32[48,96,128]{2,1,0:T(8,128)} custom-call(f32[48,96,128]{2,1,0:T(8,128)} %z_ref.1, s32[48,96]{1,0:T(8,128)} %mask_ref.1, bf16[8,2,128]{2,1,0:T(2,128)(2,1)} %bitcast.8, bf16[8,128,512]{2,1,0:T(8,128)(2,1)} %bitcast.5, bf16[8,128,128]{2,1,0:T(8,128)(2,1)} %bitcast.6, bf16[8,2,128]{2,1,0:T(2,128)(2,1)} %bitcast.9, bf16[8,128,128]{2,1,0:T(8,128)(2,1)} %bitcast.7), custom_call_target="tpu_custom_call" | custom-call | tf_op jit(solution)/shard_map/triangle_stack/pallas_call | solution.py:374
  460.2 3.2 copy.9

commit v10 on v9

--- a/solution.py
+++ b/solution.py
@@ -1,5 +1,4 @@
 import functools
-import math
 
 import jax
 import jax.numpy as jnp
@@ -15,7 +14,6 @@
 CHUNK = 16
 UNROLL = 8
 BATCH = 3
-STRIDE = 13
 MESH = pl.DeviceIdType.MESH
 
 
@@ -128,18 +126,23 @@
             body([r * CHUNK + i for i in local], local)
 
     def to_others(send_to):
-        assert math.gcd(STRIDE, n_all) == 1
+        half = n_all // 2
+
         def step(off):
-            peer = lax.rem(me + off * STRIDE, n_all)
+            peer = lax.rem(me + off, n_all)
             send_to(lax.div(peer, n_dap2), lax.rem(peer, n_dap2))
 
-        @pl.loop(0, (n_all - 1) // BATCH)
+        step(half)
+
+        @pl.loop(0, (half - 1) // BATCH)
         def _(k):
-            for s in range(BATCH):
-                step(1 + k * BATCH + s)
-
-        for off in range((n_all - 1) // BATCH * BATCH + 1, n_all):
-            step(off)
+            for s in range(1, BATCH + 1):
+                step(half + (k * BATCH + s))
+                step(half - (k * BATCH + s))
+
+        for off in range((half - 1) // BATCH * BATCH + 1, half):
+            step(half + off)
+            step(half - off)
 
     def chunk_rows(p, r):
         return pl.ds(pl.multiple_of(p * rows + r * CHUNK, CHUNK), CHUNK)

time: 464 us -> 470 us (1.013)
  Pallas kernels: 460 us -> 466 us
    pallas_call x1, Pallas kernels: 460 us -> 466 us  [local_stack(): pl.pallas_call(functools.partial(kernel, n_dap, n_dap2, n_updates), out_s...]
where the time goes in v10:
time: 470 us
  Pallas kernels  466 us (99%)
    pallas_call x1, Pallas kernels, local_stack(): pl.pallas_call(functools.partial(kernel, n_dap, n_dap2, n_updates), out_s...  466 us

profile of v10, /device:TPU:97, one launch (start us, length us, event | category | flops | bytes accessed | tf_op | source)
XLA Modules:
  0.0 469.6 jit_solution(3130466316827537188)
XLA Ops:
  0.0 466.4 %triangle_stack.1 = f32[48,96,128]{2,1,0:T(8,128)} custom-call(f32[48,96,128]{2,1,0:T(8,128)} %z_ref.1, s32[48,96]{1,0:T(8,128)} %mask_ref.1, bf16[8,2,128]{2,1,0:T(2,128)(2,1)} %bitcast.8, bf16[8,128,512]{2,1,0:T(8,128)(2,1)} %bitcast.5, bf16[8,128,128]{2,1,0:T(8,128)(2,1)} %bitcast.6, bf16[8,2,128]{2,1,0:T(2,128)(2,1)} %bitcast.9, bf16[8,128,128]{2,1,0:T(8,128)(2,1)} %bitcast.7), custom_call_target="tpu_custom_call" | custom-call | tf_op jit(solution)/shard_map/triangle_stack/pallas_call | solution.py:377
  466.4 3.2 copy.9

commit v11 on v9

--- a/solution.py
+++ b/solution.py
@@ -1,5 +1,4 @@
 import functools
-import math
 
 import jax
 import jax.numpy as jnp
@@ -15,7 +14,6 @@
 CHUNK = 16
 UNROLL = 8
 BATCH = 3
-STRIDE = 13
 MESH = pl.DeviceIdType.MESH
 
 
@@ -128,9 +126,10 @@
             body([r * CHUNK + i for i in local], local)
 
     def to_others(send_to):
-        assert math.gcd(STRIDE, n_all) == 1
+        odd = lax.rem(my_p, 2)
+
         def step(off):
-            peer = lax.rem(me + off * STRIDE, n_all)
+            peer = lax.rem(me + off + odd * (n_all - 2 * off), n_all)
             send_to(lax.div(peer, n_dap2), lax.rem(peer, n_dap2))
 
         @pl.loop(0, (n_all - 1) // BATCH)

time: 464 us -> 450 us (0.970)
  Pallas kernels: 460 us -> 446 us
    pallas_call x1, Pallas kernels: 460 us -> 446 us  [local_stack(): pl.pallas_call(functools.partial(kernel, n_dap, n_dap2, n_updates), out_s...]
where the time goes in v11:
time: 450 us
  Pallas kernels  446 us (99%)
    pallas_call x1, Pallas kernels, local_stack(): pl.pallas_call(functools.partial(kernel, n_dap, n_dap2, n_updates), out_s...  446 us

profile of v11, /device:TPU:97, one launch (start us, length us, event | category | flops | bytes accessed | tf_op | source)
XLA Modules:
  0.0 449.7 jit_solution(8566351016317911497)
XLA Ops:
  0.0 446.5 %triangle_stack.1 = f32[48,96,128]{2,1,0:T(8,128)} custom-call(f32[48,96,128]{2,1,0:T(8,128)} %z_ref.1, s32[48,96]{1,0:T(8,128)} %mask_ref.1, bf16[8,2,128]{2,1,0:T(2,128)(2,1)} %bitcast.8, bf16[8,128,512]{2,1,0:T(8,128)(2,1)} %bitcast.5, bf16[8,128,128]{2,1,0:T(8,128)(2,1)} %bitcast.6, bf16[8,2,128]{2,1,0:T(2,128)(2,1)} %bitcast.9, bf16[8,128,128]{2,1,0:T(8,128)(2,1)} %bitcast.7), custom_call_target="tpu_custom_call" | custom-call | tf_op jit(solution)/shard_map/triangle_stack/pallas_call | solution.py:373
  446.5 3.2 copy.9

commit v12 on v11

--- a/solution.py
+++ b/solution.py
@@ -172,18 +172,25 @@
         pack_chunk(r)
         send_part(parity, r, pl.ds(0, early), r * CHUNK, CHUNK)
 
-        @pl.when(r == 0)
-        def _():
-            send_part(parity, n_chunks, pl.ds(early, late), 0, CHUNK)
+        if n_chunks in parts_of(parity):
+            @pl.when(r == 0)
+            def _():
+                send_part(parity, n_chunks, pl.ds(early, late), 0, CHUNK)
 
         @pl.when(r == n_chunks - 1)
         def _():
-            send_part(parity, n_chunks + 1, pl.ds(early, late), CHUNK, rows - CHUNK)
+            send_part(parity, n_chunks + 1, pl.ds(early, late), rows - late_rows(parity), late_rows(parity))
+
+    def late_rows(parity):
+        return rows if parity else rows - CHUNK
+
+    def parts_of(parity):
+        return [part for part in range(n_chunks + 2) if not (parity and part == n_chunks)]
 
     def part_shape(parity, part):
         if part < n_chunks:
             return first_tiles(parity), CHUNK
-        return 2 * TILES - first_tiles(parity), CHUNK if part == n_chunks else rows - CHUNK
+        return 2 * TILES - first_tiles(parity), CHUNK if part == n_chunks else late_rows(parity)
 
     def wait_received(parity, part):
         tiles, n_rows = part_shape(parity, part)
@@ -280,12 +287,11 @@
                     tiles = [recv[parity, t, here, lanes].astype(jnp.float32) for t in range(TILES)]
                     bl[here, lanes] = last_group(tiles, cols).astype(jnp.bfloat16)
 
-        wait_received(parity, n_chunks)
         pl.loop(0, n_chunks)(chunk)
 
     def exchange(update, parity, contract, more):
         contract(parity)
-        for part in range(n_chunks + 2):
+        for part in parts_of(parity):
             wait_sent(parity, part)
         load_finish(update)
 

time: 450 us -> 441 us (0.980)
  Pallas kernels: 446 us -> 438 us
    pallas_call x1, Pallas kernels: 446 us -> 438 us  [local_stack(): pl.pallas_call(functools.partial(kernel, n_dap, n_dap2, n_updates), out_s...]
where the time goes in v12:
time: 441 us
  Pallas kernels  438 us (99%)
    pallas_call x1, Pallas kernels, local_stack(): pl.pallas_call(functools.partial(kernel, n_dap, n_dap2, n_updates), out_s...  438 us

profile of v12, /device:TPU:97, one launch (start us, length us, event | category | flops | bytes accessed | tf_op | source)
XLA Modules:
  0.0 441.1 jit_solution(5337058137758859124)
XLA Ops:
  0.0 437.9 %triangle_stack.1 = f32[48,96,128]{2,1,0:T(8,128)} custom-call(f32[48,96,128]{2,1,0:T(8,128)} %z_ref.1, s32[48,96]{1,0:T(8,128)} %mask_ref.1, bf16[8,2,128]{2,1,0:T(2,128)(2,1)} %bitcast.8, bf16[8,128,512]{2,1,0:T(8,128)(2,1)} %bitcast.5, bf16[8,128,128]{2,1,0:T(8,128)(2,1)} %bitcast.6, bf16[8,2,128]{2,1,0:T(2,128)(2,1)} %bitcast.9, bf16[8,128,128]{2,1,0:T(8,128)(2,1)} %bitcast.7), custom_call_target="tpu_custom_call" | custom-call | tf_op jit(solution)/shard_map/triangle_stack/pallas_call | solution.py:379
  437.9 3.2 copy.9
